TPU v7x, 32 devices: a whole 2x2x4 slice. The times are simulated.
32 devices in a mesh: dp: 2 (over core), section: 4 (over z), mp: 4 (over y, x).
Axes of the slice: x: 2, y: 2, z: 4, core: 2. Of those that a mesh axis runs over, the one named last changes fastest.
Arguments:
- inputs: bfloat16 [48, 512], P(('dp', 'mp')), may hold values from -6 to 6
- tangents: bfloat16 [48, 32, 512], P(('dp', 'mp')), may hold values from -6 to 6
- targets: bfloat16 [48, 1024], P(('dp', 'mp')), may hold values from -24 to 24
- target_jac: bfloat16 [48, 32, 1024], P(('dp', 'mp')), may hold values from -24 to 24
- rank_mask: int32 [48, 32], P(('dp', 'mp')), may hold values from 0 to 1, as said below
- batch_order: int32 [8, 6], P(('dp', 'mp')), may hold values from 0 to 5, each once within a row
- encoder: bfloat16 [512, 2048], replicated, may hold values from -0.25 to 0.25
- layers: bfloat16 [4, 2048, 2048], P('section', 'mp'), may hold values from -0.125 to 0.125
- head_weight: bfloat16 [2048, 1024], replicated, may hold values from -0.125 to 0.125
Outputs:
- grad_layers: float32 [4, 2048, 2048], P('section', ('dp', 'mp'))
- grad_head: float32 [2048, 1024], P(('dp', 'mp'), 'section')
- loss_value: float32 [], replicated
Inputs may be any that keep to these rules, and one draw needn't show every extreme that they name: `rank_mask`: each sample's ones are its first 1 to 32 directions. `batch_order`: each row is an ordering of 0 .. 5.
All inputs are finite; a program needn't handle non-finite values.
Results may differ from a plain program's by a relative error of at most 0.035.
Values may be sent and summed in bfloat16 or wider, within the bound.
No kernel may reach another device: no remote copies, remote signals or barrier semaphores. Data moves between devices by JAX's collectives and lax.ppermute only.
A program may use at most 128 MiB of HBM per device.

v0:
```python
import jax
import jax.numpy as jnp
from jax import lax
from jax.experimental import pallas as pl
from jax.experimental.pallas import tpu as pltpu
from jax.sharding import PartitionSpec as P


F32 = jnp.float32
BF16 = jnp.bfloat16
MB = 6
EXTRA = 16
BLOCKS = 4

ANY = pl.BlockSpec(memory_space=pl.ANY)
SMEM = pl.BlockSpec(memory_space=pltpu.SMEM)
VMEM = pl.BlockSpec(memory_space=pltpu.VMEM)


def round_up(value, unit):
    return -(-value // unit) * unit


def mp_swap(value, flip):
    count = lax.axis_size("mp")
    return lax.ppermute(value, "mp", [(m, m ^ flip) for m in range(count)])


def dp_swap(value):
    count = lax.axis_size("dp")
    return lax.ppermute(value, "dp", [(d, d ^ 1) for d in range(count)])


def mp_pieces(value):
    return [value] + [mp_swap(value, k) for k in range(1, lax.axis_size("mp"))]


def hop(value, source, target):
    return lax.ppermute(value, "section", [(source, target)])


def plane_pieces(value, section):
    count = lax.axis_size("mp")
    base = section * count
    swaps = [[(base + m, base + (m ^ k)) for m in range(count)] for k in range(1, count)]
    return [value] + [lax.ppermute(value, ("section", "mp"), pairs) for pairs in swaps]


def params():
    return pltpu.CompilerParams(vmem_limit_bytes=16 * 2**20)


def call(body, args, specs, deps=(), **options):
    reads, waits = len(args), len(deps)

    def inner(*refs):
        body(*refs[:reads], *refs[reads + waits :])

    return pl.pallas_call(
        inner, in_specs=list(specs) + [ANY] * waits, compiler_params=params(), **options
    )(*args, *deps)


def run_copies(copies):
    for copy in copies:
        copy.start()
    for copy in copies:
        copy.wait()


def spread(onehot, value):
    high = value.astype(BF16)
    low = (value - high.astype(F32)).astype(BF16)
    return jnp.dot(onehot, high, preferred_element_type=F32) + jnp.dot(
        onehot, low, preferred_element_type=F32
    )


class Weights:
    def __init__(self, layer):
        self.count = lax.axis_size("mp")
        self.block_rows, self.width = layer.shape
        dp_index = lax.axis_index("dp")
        half = self.block_rows // 2
        self.offsets = [dp_index * half, (1 - dp_index) * half]
        self.pieces = [(layer, 0, None, 0)]
        self.colored = self.count == 4 and lax.axis_size("dp") == 2
        self.part = part = half // 2
        if self.colored:
            self.first = lax.dynamic_slice_in_dim(layer, dp_index * half, part, 0)
            self.second = lax.dynamic_slice_in_dim(layer, dp_index * half + part, part, 0)
            self.b1 = self.swap(self.second, 1)
            self.a2 = self.swap(self.first, 2)
            self.a1 = self.swap(self.first, 1)
            self.b2 = self.swap(self.second, 2)
            self.a3 = self.swap(self.a1, 2)
            self.b3 = self.swap(self.b2, 1)
            got = [(self.a1, 1, 0), (self.b2, 2, part), (self.b1, 1, part), (self.a2, 2, 0), (self.a3, 3, 0), (self.b3, 3, part)]
            for array, block, base in got:
                self.pieces.append((array, block, 0, base))
                self.pieces.append((dp_swap(array), block, 1, base))
        else:
            for block in range(1, self.count):
                self.pieces.append((mp_swap(layer, block), block, None, 0))

    def swap(self, array, flip):
        return mp_swap(array, flip)

    def assemble(self, ids, deps):
        early = len(self.pieces) - 4 if self.colored else len(self.pieces)
        layer = self.place(ids, None, self.pieces[:early], "assemble", deps)
        return layer if early == len(self.pieces) else self.place(ids, layer, self.pieces[early:], "complete", [])

    def place(self, ids, layer, pieces, name, deps):
        many = len(pieces)

        def body(ids_ref, *refs):
            out, sems = refs[-2:]
            copies = []
            for i, (array, block, which, base) in enumerate(pieces):
                row = pl.multiple_of(ids_ref[3 + block] * self.block_rows, self.block_rows) + base
                if which is not None:
                    row = row + pl.multiple_of(ids_ref[1 + which], self.block_rows // 2)
                copies.append(
                    pltpu.make_async_copy(refs[i], out.at[pl.ds(row, array.shape[0]), :], sems.at[i])
                )
            run_copies(copies)

        before = [] if layer is None else [layer]
        return call(
            body,
            [ids, *[piece[0] for piece in pieces], *before],
            [SMEM] + [ANY] * many + [VMEM] * len(before),
            deps,
            out_shape=jax.ShapeDtypeStruct((self.count * self.block_rows, self.width), BF16),
            out_specs=VMEM,
            input_output_aliases={1 + many: 0} if before else {},
            scratch_shapes=[pltpu.SemaphoreType.DMA((many,))],
            name=name,
        )


def fwd_stage(deps, level, ids, layer, rows, onehot, slope, kept):
    height, width = rows.shape
    prims = onehot.shape[1]
    leads = slope is None
    nb = width // BLOCKS

    def body(ids_ref, layer_ref, rows_ref, onehot_ref, *rest):
        if not leads:
            slope_ref, *rest = rest
        next_ref, pre_ref, kept_ref, *rest = rest[(kept is not None) :]
        if leads:
            tanh_ref, *rest = rest
        (kept_sem,) = rest

        @pl.when(ids_ref[0] == level)
        def _():
            keep = pltpu.make_async_copy(rows_ref, kept_ref, kept_sem)
            keep.start()

            def block(n, carry):
                cols = pl.ds(pl.multiple_of(n * nb, nb), nb)
                acc = jnp.dot(rows_ref[...], layer_ref[:, cols], preferred_element_type=F32)
                old = rows_ref[:, cols].astype(F32)
                pre_ref[:, cols] = acc.astype(BF16)
                if leads:
                    tanh_p = jnp.tanh(acc[:prims])
                    tanh_ref[:, cols] = tanh_p
                    factor = spread(onehot_ref[...], 1.0 - tanh_p * tanh_p)
                    new = jnp.concatenate(
                        [old[:prims] + tanh_p, old[prims:] + factor * acc[prims:]], axis=0
                    )
                else:
                    tanh_p = slope_ref[:, cols]
                    new = old + spread(onehot_ref[...], 1.0 - tanh_p * tanh_p) * acc
                next_ref[:, cols] = new.astype(BF16)
                return carry

            lax.fori_loop(0, BLOCKS, block, 0)
            keep.wait()

    outs = [jax.ShapeDtypeStruct((height, width), BF16)] * 3
    if leads:
        outs.append(jax.ShapeDtypeStruct((prims, width), F32))
    args = [ids, layer, rows, onehot] + ([] if leads else [slope])
    specs = [SMEM] + [VMEM] * (len(args) - 1)
    alias = {}
    if kept is not None:
        alias = {len(args): 2}
        args.append(kept)
        specs.append(ANY)
    return call(
        body,
        args,
        specs,
        deps,
        out_shape=outs,
        out_specs=[VMEM, VMEM, ANY] + [VMEM] * (len(outs) - 3),
        input_output_aliases=alias,
        scratch_shapes=[pltpu.SemaphoreType.DMA],
        cost_estimate=pl.CostEstimate(flops=2 * height * width * width * 4, bytes_accessed=2 * width * width, transcendentals=0),
        name=f"fwd{level}",
    )


def bwd_stage(deps, level, ids, layer, cot, pre, tanh_p, onehot, onehot_t, total, leads, kept):
    height, width = cot.shape
    prims = tanh_p.shape[0]
    deep = level > 0
    nb = width // BLOCKS

    def body(ids_ref, cot_ref, pre_ref, tanh_ref, onehot_ref, onehot_t_ref, *rest):
        if total is not None:
            total_ref, *rest = rest
        if deep:
            layer_ref, *rest = rest
        kept_ref, side_ref, *rest = rest[(kept is not None) :]
        if deep:
            new_ref, *rest = rest
        mix_ref, kept_sem = rest

        @pl.when(ids_ref[0] == level)
        def _():
            skip = prims if leads else 0

            def block(n, carry):
                cols = pl.ds(pl.multiple_of(n * nb, nb), nb)
                up = cot_ref[:, cols].astype(F32)
                tanh = tanh_ref[:, cols]
                slope = 1.0 - tanh * tanh
                up_t = up[skip:]
                mix_t = up_t * spread(onehot_ref[...], slope)
                total_here = spread(onehot_t_ref[...], up_t * pre_ref[:, cols].astype(F32)[skip:])
                if total is not None:
                    total_here = total_here + total_ref[:, cols]
                if leads:
                    mix_p = up[:prims] * slope - 2.0 * total_here * tanh * slope
                    mix_ref[:, cols] = jnp.concatenate([mix_p, mix_t], axis=0).astype(BF16)
                else:
                    mix_ref[:, cols] = mix_t.astype(BF16)
                side_ref[:, cols] = total_here
                return carry

            lax.fori_loop(0, BLOCKS, block, 0)
            keep = pltpu.make_async_copy(mix_ref, kept_ref, kept_sem)
            keep.start()
            if deep:

                def back_block(n, carry):
                    cols = pl.ds(pl.multiple_of(n * nb, nb), nb)
                    back = lax.dot_general(
                        mix_ref[...], layer_ref[cols, :], (((1,), (1,)), ((), ())), preferred_element_type=F32
                    )
                    new_ref[:, cols] = (cot_ref[:, cols].astype(F32) + back).astype(BF16)
                    return carry

                lax.fori_loop(0, BLOCKS, back_block, 0)
            keep.wait()

    rows_shape = jax.ShapeDtypeStruct((height, width), BF16)
    outs = [rows_shape, jax.ShapeDtypeStruct((prims, width), F32)] + ([rows_shape] if deep else [])
    args = [ids, cot, pre, tanh_p, onehot, onehot_t] + ([] if total is None else [total])
    args += [layer] if deep else []
    specs = [SMEM] + [VMEM] * (len(args) - 1)
    alias = {}
    if kept is not None:
        alias = {len(args): 0}
        args.append(kept)
        specs.append(ANY)
    return call(
        body,
        args,
        specs,
        deps,
        out_shape=outs,
        out_specs=[ANY] + [VMEM] * (len(outs) - 1),
        input_output_aliases=alias,
        scratch_shapes=[pltpu.VMEM((height, width), BF16), pltpu.SemaphoreType.DMA],
        cost_estimate=pl.CostEstimate(flops=2 * height * width * width * 4, bytes_accessed=2 * width * width, transcendentals=0),
        name=f"bwd{level}",
    )


def pick_rows(deps, ids, index, pieces, level):
    height = index.shape[0]
    piece_rows, width = pieces[0].shape

    def body(ids_ref, index_ref, *rest):
        out_ref = rest[-1]

        @pl.when(ids_ref[0] == level)
        def _():
            index_here = index_ref[...]
            acc = jnp.zeros((height, width), F32)
            for k, piece_ref in enumerate(rest[:-1]):
                place = lax.broadcasted_iota(jnp.int32, (height, piece_rows), 1) + k * piece_rows
                onehot = jnp.where(place == index_here, 1.0, 0.0).astype(BF16)
                acc = acc + jnp.dot(onehot, piece_ref[...], preferred_element_type=F32)
            out_ref[...] = acc.astype(BF16)

    return call(
        body,
        [ids, index, *pieces],
        [SMEM] + [VMEM] * (1 + len(pieces)),
        deps,
        out_shape=jax.ShapeDtypeStruct((height, width), BF16),
        out_specs=VMEM,
        name="pick",
    )


def lift_rows(ids, rows, encoder, chunks):
    height = rows.shape[0] // chunks
    width = encoder.shape[1]

    def body(ids_ref, rows_ref, encoder_ref, *outs):
        @pl.when(ids_ref[0] == 0)
        def _():
            for c, out in enumerate(outs):
                part = rows_ref[c * height : (c + 1) * height, :]
                out[...] = jnp.dot(part, encoder_ref[...], preferred_element_type=F32).astype(BF16)

    return pl.pallas_call(
        body,
        out_shape=[jax.ShapeDtypeStruct((height, width), BF16)] * chunks,
        in_specs=[SMEM, VMEM, VMEM],
        out_specs=[VMEM] * chunks,
        compiler_params=params(),
        name="lift",
    )(ids, rows, encoder)


def pack_columns(deps, ids, chunks, tails, level, n_dp, n_mp, blk):
    count = len(chunks)
    height, _ = chunks[0].shape
    tail_rows, tail_width = tails[0].shape if tails else (height, 0)
    core = n_dp * blk

    def body(ids_ref, *refs):
        chunk_refs, rest = refs[:count], refs[count:]
        tail_refs, outs = rest[: len(tails)], rest[len(tails) :]

        def fill():
            for k, out in enumerate(outs):
                for c, chunk_ref in enumerate(chunk_refs):
                    first = c * tail_rows
                    for d in range(n_dp):
                        col = pl.multiple_of((ids_ref[3 + k] + d * n_mp) * blk, blk)
                        out[first : first + height, d * blk : (d + 1) * blk] = chunk_ref[:, pl.ds(col, blk)]
                    if tails:
                        out[first + height : first + tail_rows, :core] = jnp.zeros((EXTRA, core), BF16)
                        out[first : first + tail_rows, core:] = tail_refs[c][...]

        if level is None:
            fill()
        else:
            pl.when(ids_ref[0] == level)(fill)

    shape = jax.ShapeDtypeStruct((count * tail_rows, core + tail_width), BF16)
    return call(
        body,
        [ids, *chunks, *tails],
        [SMEM] + [VMEM] * (count + len(tails)),
        deps,
        out_shape=[shape] * n_mp,
        out_specs=[VMEM] * n_mp,
        name="pack",
    )


def both_groups(pieces):
    return pieces + ([dp_swap(piece) for piece in pieces] if lax.axis_size("dp") > 1 else [])


def loss_rows(loss, cols):
    high = loss.astype(BF16).astype(F32)
    line = lax.broadcasted_iota(jnp.int32, (EXTRA, cols), 0)
    return jnp.where(line == 0, high, jnp.where(line == 1, loss - high, 0.0))


def head_partial(deps, ids, pieces, level, blk, height):
    rows_each, wide = pieces[0].shape
    core = 2 * blk
    out_width = wide - core
    many = len(pieces)

    def body(ids_ref, *refs):
        piece_refs, (mine_ref, send_ref, left, right, sems) = refs[:many], refs[many:]

        @pl.when(ids_ref[0] == level)
        def _():
            here = pl.multiple_of(ids_ref[1] // ids_ref[7] * blk, blk)
            there = pl.multiple_of(blk - here, blk)
            copies = []
            for i, ref in enumerate(piece_refs):
                rows = pl.ds(i * rows_each, rows_each)
                copies.append(pltpu.make_async_copy(ref.at[:, pl.ds(here, blk)], left.at[rows, :blk], sems.at[0, i]))
                copies.append(pltpu.make_async_copy(ref.at[:, pl.ds(there, blk)], left.at[rows, blk:], sems.at[1, i]))
                copies.append(pltpu.make_async_copy(ref.at[:, core:], right.at[rows], sems.at[2, i]))
            run_copies(copies)
            loss = jnp.zeros((1, 128), F32)
            for first in range(height, many * rows_each, height + EXTRA):
                loss = loss + right[first : first + 1, :128].astype(F32) + right[first + 1 : first + 2, :128].astype(F32)
            tail = loss_rows(loss[:, :1], out_width)
            part = lax.dot_general(left[...], right[...], (((0,), (0,)), ((), ())), preferred_element_type=F32)
            mine_ref[:blk, :] = part[:blk]
            mine_ref[blk:, :] = tail
            send_ref[:blk, :] = part[blk:].astype(BF16)
            send_ref[blk:, :] = tail.astype(BF16)

    shape = (blk + EXTRA, out_width)
    return call(
        body,
        [ids, *pieces],
        [SMEM] + [ANY] * many,
        deps,
        out_shape=[jax.ShapeDtypeStruct(shape, F32), jax.ShapeDtypeStruct(shape, BF16)],
        out_specs=[VMEM] * 2,
        scratch_shapes=[
            pltpu.VMEM((many * rows_each, core), BF16),
            pltpu.VMEM((many * rows_each, out_width), BF16),
            pltpu.SemaphoreType.DMA((3, many)),
        ],
        name="head_partial",
    )


def head_gradient(deps, ids, mine, other, level, blk, n_sec):
    cols = mine.shape[1] // n_sec

    def body(ids_ref, mine_ref, other_ref, *outs):
        @pl.when(ids_ref[0] == level)
        def _():
            tails = mine_ref[blk:, :1] + other_ref[blk:, :128].astype(F32)[:, :1]
            tail = loss_rows(tails[0:1] + tails[1:2], cols).astype(BF16)
            for j, out in enumerate(outs):
                span = slice(j * cols, (j + 1) * cols)
                out[:blk, :] = (mine_ref[:blk, span] + other_ref[:blk, span].astype(F32)).astype(BF16)
                out[blk:, :] = tail

    return call(
        body,
        [ids, mine, other],
        [SMEM, VMEM, VMEM],
        deps,
        out_shape=[jax.ShapeDtypeStruct((blk + EXTRA, cols), BF16)] * n_sec,
        out_specs=[VMEM] * n_sec,
        name="grad_head",
    )


def first_gradient(deps, ids, blocks, mixes, blk, height):
    many = len(mixes)
    every = len(blocks)
    width = mixes[0].shape[1]
    nb = width // BLOCKS

    def body(ids_ref, *refs):
        block_refs, mix_refs = refs[:every], refs[every : every + many]
        mine_ref, send_ref, later_ref, left, right, early, sems = refs[every + many :]
        here = pl.multiple_of(ids_ref[1] // ids_ref[7] * blk, blk)
        there = pl.multiple_of(blk - here, blk)
        copies = []
        for i in range(every):
            rows = pl.ds(i * height, height)
            if i < many:
                for j, col in enumerate([here, there]):
                    src = block_refs[i].at[height:, pl.ds(col, blk)]
                    copies.append(pltpu.make_async_copy(src, left.at[rows, j * blk : (j + 1) * blk], sems.at[j, i]))
                copies.append(pltpu.make_async_copy(mix_refs[i], right.at[rows], sems.at[2, i]))
            src = block_refs[i].at[:height, pl.ds(here, blk)]
            copies.append(pltpu.make_async_copy(src, early.at[rows], sems.at[3, i]))
        run_copies(copies)
        later_ref[...] = early[...].astype(F32).T.astype(BF16)
        turned = left[...].astype(F32).T.astype(BF16)
        for n in range(BLOCKS):
            cols = slice(n * nb, (n + 1) * nb)
            part = jnp.dot(turned, right[:, cols], preferred_element_type=F32)
            mine_ref[:, cols] = part[:blk]
            send_ref[:, cols] = part[blk:].astype(BF16)

    return call(
        body,
        [ids, *blocks, *mixes],
        [SMEM] + [ANY] * (every + many),
        deps,
        out_shape=[
            jax.ShapeDtypeStruct((blk, width), F32),
            jax.ShapeDtypeStruct((blk, width), BF16),
            jax.ShapeDtypeStruct((blk, every * height), BF16),
        ],
        out_specs=[VMEM] * 3,
        scratch_shapes=[
            pltpu.VMEM((many * height, 2 * blk), BF16),
            pltpu.VMEM((many * height, width), BF16),
            pltpu.VMEM((every * height, blk), BF16),
            pltpu.SemaphoreType.DMA((4, every)),
        ],
        name="first_gradient",
    )


def last_gradient(deps, turned, mixes, mine, other):
    blk, width = mine.shape
    nb = width // BLOCKS

    def body(turned_ref, *refs):
        mix_refs, (mine_ref, other_ref, out) = refs[:-3], refs[-3:]
        for n in range(BLOCKS):
            cols = slice(n * nb, (n + 1) * nb)
            right = jnp.concatenate([ref[:, cols] for ref in mix_refs], axis=0)
            part = jnp.dot(turned_ref[...], right, preferred_element_type=F32)
            out[:, cols] = part + mine_ref[:, cols] + other_ref[:, cols].astype(F32)

    return call(
        body,
        [turned, *mixes, mine, other],
        [VMEM] * (3 + len(mixes)),
        deps,
        out_shape=jax.ShapeDtypeStruct((blk, width), F32),
        out_specs=VMEM,
        name="last_gradient",
    )


def join_rows(deps, flat, deep, rows_out):
    count, rank, width = deep.shape

    def body(flat_ref, deep_ref, out, sem):
        copies = [
            pltpu.make_async_copy(deep_ref.at[i], out.at[i * rank : (i + 1) * rank], sem.at[i])
            for i in range(count)
        ]
        for copy in copies:
            copy.start()
        spare = jnp.zeros((rows_out - count * (rank + 1), width), F32)
        out[count * rank :, :] = jnp.concatenate([flat_ref[...].astype(F32), spare], axis=0).astype(BF16)
        for copy in copies:
            copy.wait()

    return call(
        body,
        [flat, deep],
        [VMEM, ANY],
        deps,
        out_shape=jax.ShapeDtypeStruct((rows_out, width), BF16),
        out_specs=VMEM,
        scratch_shapes=[pltpu.SemaphoreType.DMA((count,))],
        name="join",
    )


def head_stage(deps, level, ids, rows, wanted, share, head_weight):
    height, width = rows.shape
    out_width = head_weight.shape[1]

    def body(ids_ref, rows_ref, wanted_ref, share_ref, head_ref, cot_ref, new_ref):
        @pl.when(ids_ref[0] == level)
        def _():
            nb = out_width // BLOCKS

            def block(n, loss):
                cols = pl.ds(pl.multiple_of(n * nb, nb), nb)
                outputs = jnp.dot(rows_ref[...], head_ref[:, cols], preferred_element_type=F32)
                mismatch = outputs - wanted_ref[:, cols].astype(F32)
                scaled = share_ref[...] * mismatch
                cot_ref[:height, cols] = (2.0 * scaled).astype(BF16)
                return loss + jnp.sum(scaled * mismatch, axis=1, keepdims=True)

            loss = lax.fori_loop(0, BLOCKS, block, jnp.zeros((height, 1), F32))
            loss = jnp.sum(loss, axis=0, keepdims=True)
            line = lax.broadcasted_iota(jnp.int32, (EXTRA, out_width), 0)
            high = loss.astype(BF16).astype(F32)
            tail = jnp.where(line == 0, high, jnp.where(line == 1, loss - high, 0.0))
            cot_ref[height:, :] = tail.astype(BF16)
            kb = width // BLOCKS

            def back_block(k, carry):
                cols = pl.ds(pl.multiple_of(k * kb, kb), kb)
                new_ref[:, cols] = lax.dot_general(
                    cot_ref[:height, :], head_ref[cols, :], (((1,), (1,)), ((), ())), preferred_element_type=F32
                ).astype(BF16)
                return carry

            lax.fori_loop(0, BLOCKS, back_block, 0)

    return call(
        body,
        [ids, rows, wanted, share, head_weight],
        [SMEM] + [VMEM] * 4,
        deps,
        out_shape=[
            jax.ShapeDtypeStruct((height + EXTRA, out_width), BF16),
            jax.ShapeDtypeStruct((height, width), BF16),
        ],
        out_specs=[VMEM] * 2,
        cost_estimate=pl.CostEstimate(flops=2 * height * width * width * 4, bytes_accessed=2 * width * out_width, transcendentals=0),
        name="head",
    )


def local(
    inputs, tangents, targets, target_jac, rank_mask, batch_order, encoder, layers, head_weight
):
    samp_dev, rank = rank_mask.shape
    in_width = inputs.shape[1]
    width = layers.shape[2]
    out_width = head_weight.shape[1]
    n_dp = lax.axis_size("dp")
    n_mp = lax.axis_size("mp")
    n_sec = lax.axis_size("section")
    last = n_sec - 1
    dp_index = lax.axis_index("dp")
    sec = lax.axis_index("section")
    mp_index = lax.axis_index("mp")
    prims = n_mp * samp_dev
    blk = width // (n_dp * n_mp)

    weights = Weights(layers[0])
    helper = last

    piece_rows = round_up(samp_dev * (rank + 1), 16)
    joined_rows = join_rows([], inputs, tangents, piece_rows)
    row_pieces = plane_pieces(joined_rows, helper)

    own_rank = jnp.sum(rank_mask, axis=1)
    slot_line = jnp.arange(samp_dev, dtype=jnp.int32)
    own_slot = jnp.sum(
        jnp.where(batch_order[0][None, :] == slot_line[:, None], slot_line[None, :], 0), axis=1
    ) // (samp_dev // MB)
    own_meta = jnp.stack([own_rank, own_slot]).astype(jnp.int32)
    meta_pieces = jnp.stack(mp_pieces(own_meta))
    order_line = jnp.arange(n_mp, dtype=jnp.int32)
    swap = ((order_line[:, None] ^ mp_index) == order_line[None, :]).astype(jnp.int32)
    meta = jnp.sum(swap[:, :, None, None] * meta_pieces[None], axis=1)
    ranks = meta[:, 0].reshape(prims)
    slots = meta[:, 1].reshape(prims)
    sample_line = jnp.arange(prims, dtype=jnp.int32)
    ends = jnp.sum(jnp.where(sample_line[None, :] <= sample_line[:, None], ranks[None, :], 0), axis=1)
    active = jnp.sum(ranks)
    counts = jnp.sum(jnp.where(slots[None, :] == slots[:, None], ranks[None, :] + 1, 0), axis=1)
    inverse = 1.0 / counts.astype(F32)

    kb = width // n_mp
    ids = jnp.stack(
        [sec] + weights.offsets + [mp_index ^ k for k in range(n_mp)] + [jnp.int32(kb // 2)] * (n_mp == 4)
    ).astype(jnp.int32)
    chunks = 2
    usual = samp_dev * (rank // 2 + 1)
    height = max(round_up(-(-(prims + usual) // chunks), 16), round_up(prims + 8, 16))
    slots_here = chunks * height - prims

    place = mp_index * slots_here + jnp.arange(slots_here, dtype=jnp.int32)
    passed = ends[None, :] <= place[:, None]
    sample = jnp.sum(passed.astype(jnp.int32), axis=1)
    column = place - jnp.sum(jnp.where(passed, ranks[None, :], 0), axis=1)
    present = place < active
    belongs = (sample[:, None] == sample_line[None, :]) & present[:, None]
    source = ((sample // samp_dev) ^ mp_index) * piece_rows + (sample % samp_dev) * rank + column
    source = jnp.where(present, source, -1)
    source_p = ((sample_line // samp_dev) ^ mp_index) * piece_rows + samp_dev * rank + sample_line % samp_dev
    share = jnp.sum(jnp.where(belongs, inverse[None, :], 0.0), axis=1)
    share_p = jnp.where(sample_line // samp_dev == mp_index, inverse, 0.0)
    index = jnp.concatenate([source_p, source])[:, None]
    shares = jnp.concatenate([share_p, share])[:, None]
    onehot = belongs.astype(BF16)
    first = height - prims
    onehots = [onehot[:first], onehot[first:]]
    onehot_t = ((sample_line[:, None] == sample[None, :]) & present[None, :]).astype(BF16)
    onehots_t = [onehot_t[:, :first], onehot_t[:, first:]]
    share_of = [shares[:height], shares[height:]]

    packed = pick_rows([], ids, index, row_pieces, helper)
    if helper != 0:
        packed = hop(packed, helper, 0)
    rows = list(lift_rows(ids, packed, encoder, chunks))
    other_active = dp_swap(active.reshape(1, 1)).reshape(()) if n_dp > 1 else active
    most_active = jnp.maximum(active, other_active)

    small_arrays = [*onehots, *onehots_t, *share_of, index, most_active.reshape(1)]
    layer = weights.assemble(ids, small_arrays)
    token = []
    entered = [None] * chunks
    pres = [[None] * n_sec for _ in range(chunks)]
    tanhs = [None] * n_sec
    heads = [None] * chunks
    goal_pieces = None
    for level in range(n_sec):
        for c in range(chunks):
            got = fwd_stage(
                token, level, ids, layer, rows[c], onehots[c], None if c == 0 else tanhs[level], entered[c]
            )
            token = [got[0]]
            entered[c], pres[c][level] = got[2], got[1]
            if c == 0:
                tanhs[level] = got[3]
            rows[c] = got[0] if level == last else hop(got[0], level, level + 1)
            if level == last:
                heads[c] = head_stage(
                    token, last, ids, rows[c], wanted[c * height : (c + 1) * height], share_of[c], head_weight
                )
                token = [heads[c][1]]
        if goal_pieces is None:
            goal_pieces = plane_pieces(join_rows(token, targets, target_jac, piece_rows), last)
        if level == max(last - 1, 0):
            wanted = pick_rows(token, ids, index, goal_pieces, last)
            token = [wanted]

    small = n_dp * n_mp <= 8 and blk % 128 == 0
    cots = [heads[c][1] for c in range(chunks)]
    mixes = [None] * chunks
    backward_order = list(range(1, chunks)) + [0]
    hidden_pieces = head_pieces = None
    arrived = []
    for level in range(last, -1, -1):
        total = None
        for c in backward_order:
            got = bwd_stage(
                token, level, ids, layer, cots[c], pres[c][level], tanhs[level],
                onehots[c], onehots_t[c], total, c == 0, mixes[c],
            )
            mixes[c], total = got[0], got[1]
            token = [got[1]]
            if level > 0:
                cots[c] = hop(got[2], level, level - 1)
        if not small:
            continue
        if level == last:
            sends = pack_columns(token, ids, rows, [h[0] for h in heads], last, n_dp, n_mp, blk)
            token = [sends[0]]
            base = last * n_mp
            head_pieces = [sends[0]] + [
                lax.ppermute(sends[k], ("section", "mp"), [(base + m, base + (m ^ k)) for m in range(n_mp)])
                for k in range(1, n_mp)
            ]
        elif level == last - 1:
            sends = pack_columns(token, ids, entered, [], None, n_dp, n_mp, blk)
            token = [sends[0]]
            hidden_pieces = [sends[0]] + [mp_swap(sends[k], k) for k in range(1, n_mp)]
        elif level == last - 2:
            hidden_pieces = both_groups(hidden_pieces)
            token = [*token, *hidden_pieces]

    cols = out_width // n_sec
    if small:
        swapped = []
        for c in backward_order:
            swapped.append([mixes[c]] + [mp_swap(mixes[c], k) for k in range(1, n_mp)])
        first_mine, send, turned = first_gradient([], ids, hidden_pieces, swapped[0], blk, height)
        first_other = dp_swap(send)
        mine, send = head_partial([], ids, head_pieces, last, blk, height)
        other = dp_swap(send)
        blocks = head_gradient([], ids, mine, other, last, blk, n_sec)
        arrived = [hop(blocks[j], last, j) for j in range(last)]
        head_ext = blocks[last].astype(F32)
        for j in range(last):
            head_ext = jnp.where(sec == j, arrived[j].astype(F32), head_ext)
        head_mine = head_ext[:blk]
        loss_mine = (head_ext[blk, 0] + head_ext[blk + 1, 0]) / (n_dp * MB * out_width)
        grad = last_gradient([], turned, both_groups(swapped[1]), first_mine, first_other)
    else:
        contract = (((0,), (0,)), ((), ()))
        joined = jnp.concatenate(entered, axis=0)
        part = lax.dot_general(joined, jnp.concatenate(mixes, axis=0), contract, preferred_element_type=F32)
        grad = lax.psum_scatter(part.astype(BF16), ("dp", "mp"), scatter_dimension=0, tiled=True).astype(F32)
        cot_out = jnp.concatenate([h[0][:height] for h in heads], axis=0)
        part = lax.dot_general(jnp.concatenate(rows, axis=0), cot_out, contract, preferred_element_type=F32)
        head = lax.psum_scatter(part.astype(BF16), ("dp", "mp"), scatter_dimension=0, tiled=True)
        loss = sum(jnp.sum(h[0][height : height + 2, 0].astype(F32)) for h in heads)
        loss = jnp.where(sec == last, lax.psum(loss, ("dp", "mp")), 0.0).reshape(1, 1)
        head_mine = jnp.where(sec == last, head[:, last * cols :], jnp.zeros((blk, cols), BF16))
        loss_mine = loss
        for j in range(last):
            head_mine = head_mine + hop(head[:, j * cols : (j + 1) * cols], last, j)
            loss_mine = loss_mine + hop(loss, last, j)
        head_mine = head_mine.astype(F32)
        loss_mine = loss_mine.reshape(()) / (n_dp * MB * out_width)
    fast = (grad[None], head_mine, loss_mine)

    def plain():
        depth = rank + 1
        total_rows = samp_dev * depth
        layer_full = jnp.zeros((width, width), BF16)
        kb = weights.block_rows
        for array, block, which, base in weights.pieces:
            row = (mp_index ^ block) * kb + base
            row = row if which is None else row + weights.offsets[which]
            layer_full = lax.dynamic_update_slice_in_dim(layer_full, array, row, 0)
        rows_in = jnp.concatenate([inputs[:, None, :], tangents], axis=1).reshape(total_rows, in_width)
        start = jnp.dot(rows_in, encoder, preferred_element_type=F32).astype(BF16)
        chain = [(j, (j + 1) % n_sec) for j in range(n_sec)]

        def back_one(value):
            return lax.fori_loop(0, last, lambda _, v: lax.ppermute(v, "section", chain), value)

        def pre_of(rows):
            pre = jnp.dot(rows, layer_full, preferred_element_type=F32).reshape(samp_dev, depth, width)
            tanh_p = jnp.tanh(pre[:, 0])
            return pre, tanh_p, 1.0 - tanh_p * tanh_p

        def forward(level, state):
            rows, mine, _ = state
            mine = jnp.where(level == sec, rows, mine)
            pre, tanh_p, slope = pre_of(rows)
            change = jnp.concatenate([tanh_p[:, None], slope[:, None] * pre[:, 1:]], axis=1)
            new = (rows.astype(F32) + change.reshape(total_rows, width)).astype(BF16)
            return lax.ppermute(new, "section", chain), mine, new

        _, mine, final = lax.fori_loop(0, n_sec, forward, (start, start, start))
        own = lax.dynamic_slice_in_dim(inverse, mp_index * samp_dev, samp_dev, 0)
        row_weight = jnp.concatenate([jnp.ones((samp_dev, 1), F32), rank_mask.astype(F32)], axis=1)
        share = (row_weight * own[:, None]).reshape(total_rows, 1)
        outputs = jnp.dot(final, head_weight, preferred_element_type=F32)
        wanted = jnp.concatenate([targets[:, None, :], target_jac], axis=1).reshape(total_rows, out_width)
        mismatch = outputs - wanted.astype(F32)
        loss = jnp.sum(share * mismatch * mismatch)
        cot_out = (2.0 * share * mismatch).astype(BF16)
        cot = lax.dot_general(cot_out, head_weight, (((1,), (1,)), ((), ())), preferred_element_type=F32)
        pre, tanh_p, slope = pre_of(mine)

        def backward(step, state):
            cot, mix_mine = state
            up = cot.astype(F32).reshape(samp_dev, depth, width)
            side = jnp.sum(up[:, 1:] * pre[:, 1:], axis=1)
            lead = up[:, 0] * slope - 2.0 * side * tanh_p * slope
            mix = jnp.concatenate([lead[:, None], up[:, 1:] * slope[:, None]], axis=1)
            mix = mix.astype(BF16).reshape(total_rows, width)
            mix_mine = jnp.where(step == last - sec, mix, mix_mine)
            back = lax.dot_general(mix, layer_full, (((1,), (1,)), ((), ())), preferred_element_type=F32)
            new = (up.reshape(total_rows, width) + back).astype(BF16)
            return back_one(new), mix_mine

        _, mix = lax.fori_loop(0, n_sec, backward, (cot.astype(BF16), mine))

        def scatter(left, right):
            part = lax.dot_general(left, right, (((0,), (0,)), ((), ())), preferred_element_type=F32)
            part = part.astype(BF16).reshape(n_dp, n_mp, blk, right.shape[1])
            mine_part = jnp.zeros((n_dp, blk, right.shape[1]), F32)
            for k in range(n_mp):
                piece = lax.dynamic_index_in_dim(part, mp_index ^ k, 1, False)
                mine_part = mine_part + (piece if k == 0 else mp_swap(piece, k)).astype(F32)
            kept = lax.dynamic_index_in_dim(mine_part, dp_index, 0, False)
            if n_dp > 1:
                sent = lax.dynamic_index_in_dim(mine_part, 1 - dp_index, 0, False)
                kept = kept + dp_swap(sent.astype(BF16)).astype(F32)
            return kept

        grad = scatter(mine, mix)
        head = scatter(final, cot_out)
        cols = out_width // n_sec
        loss_group = sum(mp_pieces(loss.reshape(1, 1)))
        if n_dp > 1:
            loss_group = loss_group + dp_swap(loss_group)
        head_mine = jnp.where(sec == last, head[:, last * cols :], 0.0)
        loss_mine = jnp.where(sec == last, loss_group, 0.0)
        for j in range(last):
            block = jnp.concatenate([head[:, j * cols : (j + 1) * cols], jnp.broadcast_to(loss_group, (8, cols))])
            block = hop(block, last, j)
            head_mine = head_mine + block[:blk]
            loss_mine = loss_mine + block[blk:, :1][:1]
        return grad[None], head_mine, loss_mine.reshape(()) / (n_dp * MB * out_width)

    room = n_mp * slots_here
    if room >= n_mp * samp_dev * rank:
        return fast
    return lax.while_loop(
        lambda state: state[0] > room, lambda state: (jnp.int32(0), *plain()), (most_active, *fast)
    )[1:]


def solution(mesh):
    in_specs = (
        P(("dp", "mp"), None),
        P(("dp", "mp"), None, None),
        P(("dp", "mp"), None),
        P(("dp", "mp"), None, None),
        P(("dp", "mp"), None),
        P(("dp", "mp"), None),
        P(),
        P("section", "mp", None),
        P(),
    )
    out_specs = (P("section", ("dp", "mp"), None), P(("dp", "mp"), "section"), P())

    return jax.shard_map(local, mesh=mesh, in_specs=in_specs, out_specs=out_specs, check_vma=False)
```

profile of v0, /device:TPU:0, one launch (start us, length us, event | category | flops | bytes accessed | tf_op | source)
XLA Modules:
  0.0 223.3 jit_solution(3781995527134998296)
XLA Ops:
  2.4 3.0 %collective-permute-start.17 = (s32[2,6]{1,0:T(2,128)S(1)}, s32[2,6]{1,0:T(2,128)S(1)}, u32[]{:S(2)}, u32[]{:S(2)}) collective-permute-start(s32[2,6]{1,0:T(2,128)S(1)} %get-tuple-element.748), channel_id=1, source_target_pairs={{0,1},{1,0},{2,3},{3,2},{4,5},{5,4},{6,7},{7,6},{8,9},{9,8},{10,11... | collective-permute-start | bytes 152 | tf_op jit(solution)/shard_map/ppermute | solution.py:26
  5.4 1.5 collective-permute-start.18
  6.9 1.6 join.2.refs_2_
  9.3 2.3 %dynamic-slice_bitcast_fusion.6 = (bf16[128,2048]{1,0:T(8,128)(2,1)}, bf16[128,2048]{1,0:T(8,128)(2,1)}) fusion(bf16[1,512,2048]{2,1,0:T(8,128)(2,1)} %param.24, s32[]{:T(128)S(6)} %select_n.205, s32[]{:T(128)S(6)} %select_n.204), kind=kLoop, calls=%fused_computation.55 | loop fusion | bytes 2097160 | tf_op jit(solution)/shard_map/dynamic_slice | solution.py:91
  12.4 2.0 collective-permute-start.21
  14.4 1.5 collective-permute-start.24
  22.7 4.9 %collective-permute-done.21.refs_2_ = bf16[128,2048]{1,0:T(8,128)(2,1)} collective-permute-done((bf16[128,2048]{1,0:T(8,128)(2,1)}, bf16[128,2048]{1,0:T(8,128)(2,1)}, u32[]{:S(2)}, u32[]{:S(2)}) %collective-permute-start.21) | collective-permute-done | bytes 524320 | tf_op jit(solution)/shard_map/ppermute | solution.py:26
  27.6 19.1 %collective-permute-done.36.rows_ref = bf16[128,512]{1,0:T(8,128)(2,1)S(1)} collective-permute-done((bf16[128,512]{1,0:T(8,128)(2,1)S(1)}, bf16[128,512]{1,0:T(8,128)(2,1)S(1)}, u32[]{:S(2)}, u32[]{:S(2)}) %collective-permute-start.36) | collective-permute-done | bytes 131104 | tf_op jit(solution)/shard_map/ppermute | solution.py:39
  46.6 1.5 collective-permute-start.22
  50.4 5.7 %collective-permute-done.22.refs_1_ = bf16[128,2048]{1,0:T(8,128)(2,1)} collective-permute-done((bf16[128,2048]{1,0:T(8,128)(2,1)}, bf16[128,2048]{1,0:T(8,128)(2,1)}, u32[]{:S(2)}, u32[]{:S(2)}) %collective-permute-start.22) | collective-permute-done | bytes 524320 | tf_op jit(solution)/shard_map/ppermute | solution.py:26
  56.1 1.5 collective-permute-done.25.refs_3_
  59.4 2.4 %lift.1 = (bf16[64,2048]{1,0:T(8,128)(2,1)S(1)}, bf16[64,2048]{1,0:T(8,128)(2,1)S(1)}) custom-call(s32[8]{0:T(128)S(1)} %stack.60.refs_0_.ids_ref, bf16[128,512]{1,0:T(8,128)(2,1)S(1)} %collective-permute-done.36.rows_ref, bf16[512,2048]{1,0:T(8,128)(2,1)} %encoder_ref.1), custom_call_target="tpu_custom_call" | custom-call | tf_op jit(solution)/shard_map/lift/pallas_call | solution.py:324
  61.9 2.8 %assemble.1.refs_5_ = bf16[2048,2048]{1,0:T(8,128)(2,1)S(1)} custom-call(s32[8]{0:T(128)S(1)} %stack.60.refs_0_.ids_ref, bf16[512,2048]{1,0:T(8,128)(2,1)S(1)} %bitcast.126, bf16[128,2048]{1,0:T(8,128)(2,1)} %collective-permute-done.21.refs_2_, bf16[128,2048]{1,0:T(8,128)(2,1)} %copy-done.20, bf16[128,2048]{1,0:T(8,128)(2,1)} %collective-permute-done.24.refs_4_, ...), custom_call_target="tpu_custom_call" | custom-call | tf_op jit(solution)/shard_map/assemble/pallas_call | solution.py:59
  64.7 2.1 complete.1.refs_1_.refs_6_.refs_7_
  66.8 3.2 %fwd0.2 = (bf16[64,2048]{1,0:T(8,128)(2,1)S(1)}, bf16[64,2048]{1,0:T(8,128)(2,1)S(1)}, bf16[64,2048]{1,0:T(8,128)(2,1)S(1)}, f32[24,2048]{1,0:T(8,128)S(1)}) custom-call(s32[8]{0:T(128)S(1)} %stack.60.refs_0_.ids_ref, bf16[2048,2048]{1,0:T(8,128)(2,1)S(1)} %complete.1.refs_1_.refs_6_.refs_7_, bf16[64,2048]{1,0:T(8,128)(2,1)S(1)} %get-tuple-element.552.refs_2_, ...), custom_call_target="tpu_custom_call" | custom-call | flops 2147483648 | bytes 8388608 | tf_op jit(solution)/shard_map/fwd0/pallas_call | solution.py:59
  71.3 2.7 %fwd0.3 = (bf16[64,2048]{1,0:T(8,128)(2,1)S(1)}, bf16[64,2048]{1,0:T(8,128)(2,1)S(1)}, bf16[64,2048]{1,0:T(8,128)(2,1)S(1)}) custom-call(s32[8]{0:T(128)S(1)} %stack.60.refs_0_.ids_ref, bf16[2048,2048]{1,0:T(8,128)(2,1)S(1)} %complete.1.refs_1_.refs_6_.refs_7_, bf16[64,2048]{1,0:T(8,128)(2,1)S(1)} %get-tuple-element.555.refs_2_, ...), custom_call_target="tpu_custom_call" | custom-call | flops 2147483648 | bytes 8388608 | tf_op jit(solution)/shard_map/fwd0/pallas_call | solution.py:59
  75.3 2.6 %collective-permute-done.37.refs_2_ = bf16[64,2048]{1,0:T(8,128)(2,1)S(1)} collective-permute-done((bf16[64,2048]{1,0:T(8,128)(2,1)S(1)}, bf16[64,2048]{1,0:T(8,128)(2,1)S(1)}, u32[]{:S(2)}, u32[]{:S(2)}) %collective-permute-start.37) | collective-permute-done | bytes 262176 | tf_op jit(solution)/shard_map/ppermute | solution.py:39
  79.2 4.2 %collective-permute-done.39.refs_2_ = bf16[64,2048]{1,0:T(8,128)(2,1)S(1)} collective-permute-done((bf16[64,2048]{1,0:T(8,128)(2,1)S(1)}, bf16[64,2048]{1,0:T(8,128)(2,1)S(1)}, u32[]{:S(2)}, u32[]{:S(2)}) %collective-permute-start.39) | collective-permute-done | bytes 262176 | tf_op jit(solution)/shard_map/ppermute | solution.py:39
  91.0 1.6 copy-done.9
  101.0 2.4 %collective-permute-start.50 = (bf16[128,512]{1,0:T(8,128)(2,1)S(1)}, bf16[128,512]{1,0:T(8,128)(2,1)S(1)}, u32[]{:S(2)}, u32[]{:S(2)}) collective-permute-start(bf16[128,512]{1,0:T(8,128)(2,1)S(1)} %get-tuple-element.594), channel_id=1, source_target_pairs={{0,3},{1,2},{2,1},{3,0},{4,7},{5,6},{6,5},{7,4},{8,11},{9,10},{10,... | collective-permute-start | bytes 393224 | tf_op jit(solution)/shard_map/ppermute | solution.py:26
  104.1 2.2 collective-permute-done.48.refs_9_.refs_2_
  114.0 45.2 %collective-permute-done.56.refs_1_ = bf16[64,2048]{1,0:T(8,128)(2,1)S(1)} collective-permute-done((bf16[64,2048]{1,0:T(8,128)(2,1)S(1)}, bf16[64,2048]{1,0:T(8,128)(2,1)S(1)}, u32[]{:S(2)}, u32[]{:S(2)}) %collective-permute-start.56) | collective-permute-done | bytes 262176 | tf_op jit(solution)/shard_map/ppermute | solution.py:39
  160.6 2.9 %collective-permute-start.58 = (bf16[64,2048]{1,0:T(8,128)(2,1)S(1)}, bf16[64,2048]{1,0:T(8,128)(2,1)S(1)}, u32[]{:S(2)}, u32[]{:S(2)}) collective-permute-start(bf16[64,2048]{1,0:T(8,128)(2,1)S(1)} %get-tuple-element.606.refs_9_), channel_id=1, source_target_pairs={{0,1},{1,0},{2,3},{3,2},{4,5},{5,4},{6,7},{7,6},{8,9},{9,8},{10,11... | collective-permute-start | bytes 786440 | tf_op jit(solution)/shard_map/ppermute | solution.py:26
  163.5 1.5 collective-permute-start.59
  167.1 3.6 %collective-permute-done.58.refs_10_ = bf16[64,2048]{1,0:T(8,128)(2,1)S(1)} collective-permute-done((bf16[64,2048]{1,0:T(8,128)(2,1)S(1)}, bf16[64,2048]{1,0:T(8,128)(2,1)S(1)}, u32[]{:S(2)}, u32[]{:S(2)}) %collective-permute-start.58) | collective-permute-done | bytes 262176 | tf_op jit(solution)/shard_map/ppermute | solution.py:26
  170.6 6.3 %collective-permute-done.59.refs_11_ = bf16[64,2048]{1,0:T(8,128)(2,1)S(1)} collective-permute-done((bf16[64,2048]{1,0:T(8,128)(2,1)S(1)}, bf16[64,2048]{1,0:T(8,128)(2,1)S(1)}, u32[]{:S(2)}, u32[]{:S(2)}) %collective-permute-start.59) | collective-permute-done | bytes 262176 | tf_op jit(solution)/shard_map/ppermute | solution.py:26
  177.0 2.8 %first_gradient.1 = (f32[256,2048]{1,0:T(8,128)S(1)}, bf16[256,2048]{1,0:T(8,128)(2,1)}, bf16[256,512]{1,0:T(8,128)(2,1)S(1)}) custom-call(s32[8]{0:T(128)S(1)} %stack.60.refs_0_.ids_ref, bf16[128,512]{1,0:T(8,128)(2,1)S(1)} %get-tuple-element.591.refs_8_.refs_1_, bf16[128,512]{1,0:T(8,128)(2,1)S(1)} %collective-permute-done.48.refs_9_.refs_2_, ...), custom_call_target="tpu_custom_call" | custom-call | tf_op jit(solution)/shard_map/first_gradient/pallas_call | solution.py:59
  179.8 2.0 bwd0.3
  188.7 2.4 %collective-permute-done.62.refs_2_ = bf16[64,2048]{1,0:T(8,128)(2,1)S(1)} collective-permute-done((bf16[64,2048]{1,0:T(8,128)(2,1)S(1)}, bf16[64,2048]{1,0:T(8,128)(2,1)S(1)}, u32[]{:S(2)}, u32[]{:S(2)}) %collective-permute-start.62) | collective-permute-done | bytes 262176 | tf_op jit(solution)/shard_map/ppermute | solution.py:26
  192.5 3.1 %collective-permute-done.63.refs_3_ = bf16[64,2048]{1,0:T(8,128)(2,1)S(1)} collective-permute-done((bf16[64,2048]{1,0:T(8,128)(2,1)S(1)}, bf16[64,2048]{1,0:T(8,128)(2,1)S(1)}, u32[]{:S(2)}, u32[]{:S(2)}) %collective-permute-start.63) | collective-permute-done | bytes 262176 | tf_op jit(solution)/shard_map/ppermute | solution.py:26
  198.3 14.3 %collective-permute-done.76 = bf16[272,256]{1,0:T(8,128)(2,1)} collective-permute-done((bf16[272,256]{1,0:T(8,128)(2,1)}, bf16[272,256]{1,0:T(8,128)(2,1)}, u32[]{:S(2)}, u32[]{:S(2)}) %collective-permute-start.76) | collective-permute-done | bytes 139296 | tf_op jit(solution)/shard_map/ppermute | solution.py:39
  219.2 3.0 %last_gradient.1 = f32[256,2048]{1,0:T(8,128)} custom-call(bf16[256,512]{1,0:T(8,128)(2,1)S(1)} %copy-done.1, bf16[64,2048]{1,0:T(8,128)(2,1)S(1)} %get-tuple-element.612.refs_1_, bf16[64,2048]{1,0:T(8,128)(2,1)S(1)} %copy-done.3, bf16[64,2048]{1,0:T(8,128)(2,1)S(1)} %copy-done.5, bf16[64,2048]{1,0:T(8,128)(2,1)} %collective-permute-done.64.refs_4_, ...), custom_call_target="tpu_custom_call" | custom-call | tf_op jit(solution)/shard_map/last_gradient/pallas_call | solution.py:59
  (187 shorter events, 60.0 us)
Async XLA Ops:
  2.4 10.0 %collective-permute-start.17 = (s32[2,6]{1,0:T(2,128)S(1)}, s32[2,6]{1,0:T(2,128)S(1)}, u32[]{:S(2)}, u32[]{:S(2)}) collective-permute-start(s32[2,6]{1,0:T(2,128)S(1)} %get-tuple-element.748), channel_id=1, source_target_pairs={{0,1},{1,0},{2,3},{3,2},{4,5},{5,4},{6,7},{7,6},{8,9},{9,8},{10,11... | collective-permute-start | bytes 152 | tf_op jit(solution)/shard_map/ppermute | solution.py:26
  8.5 10.2 %collective-permute-start.33 = (bf16[208,512]{1,0:T(8,128)(2,1)S(1)}, bf16[208,512]{1,0:T(8,128)(2,1)S(1)}, u32[]{:S(2)}, u32[]{:S(2)}) collective-permute-start(bf16[208,512]{1,0:T(8,128)(2,1)S(1)} %join.2.refs_2_), channel_id=1, source_target_pairs={{12,13},{13,12},{14,15},{15,14},{28,29},{29,28},{30,31},{31,30}} | collective-permute-start | bytes 638984 | tf_op jit(solution)/shard_map/ppermute | solution.py:46
  12.4 15.2 %collective-permute-start.21 = (bf16[128,2048]{1,0:T(8,128)(2,1)}, bf16[128,2048]{1,0:T(8,128)(2,1)}, u32[]{:S(2)}, u32[]{:S(2)}) collective-permute-start(bf16[128,2048]{1,0:T(8,128)(2,1)} %get-tuple-element.742), channel_id=1, source_target_pairs={{0,1},{1,0},{2,3},{3,2},{4,5},{5,4},{6,7},{7,6},{8,9},{9,8},{10,11... | collective-permute-start | bytes 1572872 | tf_op jit(solution)/shard_map/ppermute | solution.py:26
  14.4 33.8 %collective-permute-start.24 = (bf16[128,2048]{1,0:T(8,128)(2,1)}, bf16[128,2048]{1,0:T(8,128)(2,1)}, u32[]{:S(2)}, u32[]{:S(2)}) collective-permute-start(bf16[128,2048]{1,0:T(8,128)(2,1)} %get-tuple-element.741), channel_id=1, source_target_pairs={{0,2},{1,3},{2,0},{3,1},{4,6},{5,7},{6,4},{7,5},{8,10},{9,11},{10,... | collective-permute-start | bytes 1572872 | tf_op jit(solution)/shard_map/ppermute | solution.py:26
  18.8 30.9 %collective-permute-start.29 = (bf16[128,2048]{1,0:T(8,128)(2,1)}, bf16[128,2048]{1,0:T(8,128)(2,1)}, u32[]{:S(2)}, u32[]{:S(2)}) collective-permute-start(bf16[128,2048]{1,0:T(8,128)(2,1)} %get-tuple-element.741), channel_id=1, source_target_pairs={{0,1},{1,0},{2,3},{3,2},{4,5},{5,4},{6,7},{7,6},{8,9},{9,8},{10,11... | collective-permute-start | bytes 1572872 | tf_op jit(solution)/shard_map/ppermute | solution.py:26
  19.9 26.7 %collective-permute-start.36 = (bf16[128,512]{1,0:T(8,128)(2,1)S(1)}, bf16[128,512]{1,0:T(8,128)(2,1)S(1)}, u32[]{:S(2)}, u32[]{:S(2)}) collective-permute-start(bf16[128,512]{1,0:T(8,128)(2,1)S(1)} %pick.2), channel_id=1, source_target_pairs={{12,0},{13,1},{14,2},{15,3},{28,16},{29,17},{30,18},{31,19}} | collective-permute-start | bytes 393224 | tf_op jit(solution)/shard_map/ppermute | solution.py:39
  22.6 27.2 %collective-permute-start.31 = (bf16[128,2048]{1,0:T(8,128)(2,1)}, bf16[128,2048]{1,0:T(8,128)(2,1)S(1)}, u32[]{:S(2)}, u32[]{:S(2)}) collective-permute-start(bf16[128,2048]{1,0:T(8,128)(2,1)} %get-tuple-element.742), channel_id=1, source_target_pairs={{0,2},{1,3},{2,0},{3,1},{4,6},{5,7},{6,4},{7,5},{8,10},{9,11},{10,... | collective-permute-start | bytes 1572872 | tf_op jit(solution)/shard_map/ppermute | solution.py:26
  27.6 22.7 %collective-permute-start.27 = (bf16[128,2048]{1,0:T(8,128)(2,1)}, bf16[128,2048]{1,0:T(8,128)(2,1)S(1)}, u32[]{:S(2)}, u32[]{:S(2)}) collective-permute-start(bf16[128,2048]{1,0:T(8,128)(2,1)} %collective-permute-done.21.refs_2_), channel_id=1, source_target_pairs={{0,16},{16,0},{1,17},{17,1},{2,18},{18,2},{3,19},{19,3},{4,20},{20... | collective-permute-start | bytes 1572872 | tf_op jit(solution)/shard_map/ppermute | solution.py:31
  46.6 9.5 %collective-permute-start.22 = (bf16[128,2048]{1,0:T(8,128)(2,1)}, bf16[128,2048]{1,0:T(8,128)(2,1)}, u32[]{:S(2)}, u32[]{:S(2)}) collective-permute-start(bf16[128,2048]{1,0:T(8,128)(2,1)} %collective-permute-done.21.refs_2_), channel_id=1, source_target_pairs={{0,2},{1,3},{2,0},{3,1},{4,6},{5,7},{6,4},{7,5},{8,10},{9,11},{10,... | collective-permute-start | bytes 1572872 | tf_op jit(solution)/shard_map/ppermute | solution.py:26
  48.2 9.5 %collective-permute-start.25 = (bf16[128,2048]{1,0:T(8,128)(2,1)}, bf16[128,2048]{1,0:T(8,128)(2,1)}, u32[]{:S(2)}, u32[]{:S(2)}) collective-permute-start(bf16[128,2048]{1,0:T(8,128)(2,1)} %collective-permute-done.24.refs_4_), channel_id=1, source_target_pairs={{0,1},{1,0},{2,3},{3,2},{4,5},{5,4},{6,7},{7,6},{8,9},{9,8},{10,11... | collective-permute-start | bytes 1572872 | tf_op jit(solution)/shard_map/ppermute | solution.py:26
  49.7 12.1 %collective-permute-start.28 = (bf16[128,2048]{1,0:T(8,128)(2,1)}, bf16[128,2048]{1,0:T(8,128)(2,1)}, u32[]{:S(2)}, u32[]{:S(2)}) collective-permute-start(bf16[128,2048]{1,0:T(8,128)(2,1)} %collective-permute-done.24.refs_4_), channel_id=1, source_target_pairs={{0,16},{16,0},{1,17},{17,1},{2,18},{18,2},{3,19},{19,3},{4,20},{20... | collective-permute-start | bytes 1572872 | tf_op jit(solution)/shard_map/ppermute | solution.py:31
  49.8 12.0 %collective-permute-start.30 = (bf16[128,2048]{1,0:T(8,128)(2,1)}, bf16[128,2048]{1,0:T(8,128)(2,1)}, u32[]{:S(2)}, u32[]{:S(2)}) collective-permute-start(bf16[128,2048]{1,0:T(8,128)(2,1)} %collective-permute-done.29.refs_6_), channel_id=1, source_target_pairs={{0,16},{16,0},{1,17},{17,1},{2,18},{18,2},{3,19},{19,3},{4,20},{20... | collective-permute-start | bytes 1572872 | tf_op jit(solution)/shard_map/ppermute | solution.py:31
  50.3 11.5 %collective-permute-start.32 = (bf16[128,2048]{1,0:T(8,128)(2,1)S(1)}, bf16[128,2048]{1,0:T(8,128)(2,1)}, u32[]{:S(2)}, u32[]{:S(2)}) collective-permute-start(bf16[128,2048]{1,0:T(8,128)(2,1)S(1)} %collective-permute-done.31.refs_8_), channel_id=1, source_target_pairs={{0,16},{16,0},{1,17},{17,1},{2,18},{18,2},{3,19},{19,3},{4,20},{20... | collective-permute-start | bytes 1572872 | tf_op jit(solution)/shard_map/ppermute | solution.py:31
  74.0 9.3 %collective-permute-start.39 = (bf16[64,2048]{1,0:T(8,128)(2,1)S(1)}, bf16[64,2048]{1,0:T(8,128)(2,1)S(1)}, u32[]{:S(2)}, u32[]{:S(2)}) collective-permute-start(bf16[64,2048]{1,0:T(8,128)(2,1)S(1)} %get-tuple-element.557.refs_5_.refs_2_), channel_id=1, source_target_pairs={{0,4},{1,5},{2,6},{3,7},{16,20},{17,21},{18,22},{19,23}} | collective-permute-start | bytes 786440 | tf_op jit(solution)/shard_map/ppermute | solution.py:39
  98.0 10.9 %collective-permute-start.55 = (bf16[64,2048]{1,0:T(8,128)(2,1)S(1)}, bf16[64,2048]{1,0:T(8,128)(2,1)S(1)}, u32[]{:S(2)}, u32[]{:S(2)}) collective-permute-start(bf16[64,2048]{1,0:T(8,128)(2,1)S(1)} %get-tuple-element.595), channel_id=1, source_target_pairs={{8,4},{9,5},{10,6},{11,7},{24,20},{25,21},{26,22},{27,23}} | collective-permute-start | bytes 786440 | tf_op jit(solution)/shard_map/ppermute | solution.py:39
  106.3 58.7 %collective-permute-start.70 = (bf16[160,1536]{1,0:T(8,128)(2,1)S(1)}, bf16[160,1536]{1,0:T(8,128)(2,1)S(1)}, u32[]{:S(2)}, u32[]{:S(2)}) collective-permute-start(bf16[160,1536]{1,0:T(8,128)(2,1)S(1)} %get-tuple-element.615), channel_id=1, source_target_pairs={{12,13},{13,12},{14,15},{15,14},{28,29},{29,28},{30,31},{31,30}} | collective-permute-start | bytes 1474568 | tf_op jit(solution)/shard_map/ppermute | solution.py:734
  109.8 49.4 %collective-permute-start.56 = (bf16[64,2048]{1,0:T(8,128)(2,1)S(1)}, bf16[64,2048]{1,0:T(8,128)(2,1)S(1)}, u32[]{:S(2)}, u32[]{:S(2)}) collective-permute-start(bf16[64,2048]{1,0:T(8,128)(2,1)S(1)} %get-tuple-element.598), channel_id=1, source_target_pairs={{4,0},{5,1},{6,2},{7,3},{20,16},{21,17},{22,18},{23,19}} | collective-permute-start | bytes 786440 | tf_op jit(solution)/shard_map/ppermute | solution.py:39
  111.1 53.9 %collective-permute-start.71 = (bf16[160,1536]{1,0:T(8,128)(2,1)S(1)}, bf16[160,1536]{1,0:T(8,128)(2,1)S(1)}, u32[]{:S(2)}, u32[]{:S(2)}) collective-permute-start(bf16[160,1536]{1,0:T(8,128)(2,1)S(1)} %get-tuple-element.616), channel_id=1, source_target_pairs={{12,14},{13,15},{14,12},{15,13},{28,30},{29,31},{30,28},{31,29}} | collective-permute-start | bytes 1474568 | tf_op jit(solution)/shard_map/ppermute | solution.py:734
  111.8 54.5 %collective-permute-start.72 = (bf16[160,1536]{1,0:T(8,128)(2,1)S(1)}, bf16[160,1536]{1,0:T(8,128)(2,1)S(1)}, u32[]{:S(2)}, u32[]{:S(2)}) collective-permute-start(bf16[160,1536]{1,0:T(8,128)(2,1)S(1)} %get-tuple-element.617), channel_id=1, source_target_pairs={{12,15},{13,14},{14,13},{15,12},{28,31},{29,30},{30,29},{31,28}} | collective-permute-start | bytes 1474568 | tf_op jit(solution)/shard_map/ppermute | solution.py:734
  160.6 10.0 %collective-permute-start.58 = (bf16[64,2048]{1,0:T(8,128)(2,1)S(1)}, bf16[64,2048]{1,0:T(8,128)(2,1)S(1)}, u32[]{:S(2)}, u32[]{:S(2)}) collective-permute-start(bf16[64,2048]{1,0:T(8,128)(2,1)S(1)} %get-tuple-element.606.refs_9_), channel_id=1, source_target_pairs={{0,1},{1,0},{2,3},{3,2},{4,5},{5,4},{6,7},{7,6},{8,9},{9,8},{10,11... | collective-permute-start | bytes 786440 | tf_op jit(solution)/shard_map/ppermute | solution.py:26
  163.5 13.5 %collective-permute-start.59 = (bf16[64,2048]{1,0:T(8,128)(2,1)S(1)}, bf16[64,2048]{1,0:T(8,128)(2,1)S(1)}, u32[]{:S(2)}, u32[]{:S(2)}) collective-permute-start(bf16[64,2048]{1,0:T(8,128)(2,1)S(1)} %get-tuple-element.606.refs_9_), channel_id=1, source_target_pairs={{0,2},{1,3},{2,0},{3,1},{4,6},{5,7},{6,4},{7,5},{8,10},{9,11},{10,... | collective-permute-start | bytes 786440 | tf_op jit(solution)/shard_map/ppermute | solution.py:26
  165.0 12.0 %collective-permute-start.60 = (bf16[64,2048]{1,0:T(8,128)(2,1)S(1)}, bf16[64,2048]{1,0:T(8,128)(2,1)S(1)}, u32[]{:S(2)}, u32[]{:S(2)}) collective-permute-start(bf16[64,2048]{1,0:T(8,128)(2,1)S(1)} %get-tuple-element.606.refs_9_), channel_id=1, source_target_pairs={{0,3},{1,2},{2,1},{3,0},{4,7},{5,6},{6,5},{7,4},{8,11},{9,10},{10,... | collective-permute-start | bytes 786440 | tf_op jit(solution)/shard_map/ppermute | solution.py:26
  165.0 14.8 %collective-permute-start.61 = (bf16[64,2048]{1,0:T(8,128)(2,1)S(1)}, bf16[64,2048]{1,0:T(8,128)(2,1)S(1)}, u32[]{:S(2)}, u32[]{:S(2)}) collective-permute-start(bf16[64,2048]{1,0:T(8,128)(2,1)S(1)} %get-tuple-element.608), channel_id=1, source_target_pairs={{4,0},{5,1},{6,2},{7,3},{20,16},{21,17},{22,18},{23,19}} | collective-permute-start | bytes 786440 | tf_op jit(solution)/shard_map/ppermute | solution.py:39
  167.0 18.5 %collective-permute-start.73 = (bf16[272,1024]{1,0:T(8,128)(2,1)S(1)}, bf16[272,1024]{1,0:T(8,128)(2,1)S(1)}, u32[]{:S(2)}, u32[]{:S(2)}) collective-permute-start(bf16[272,1024]{1,0:T(8,128)(2,1)S(1)} %get-tuple-element.619), channel_id=1, source_target_pairs={{0,16},{16,0},{1,17},{17,1},{2,18},{18,2},{3,19},{19,3},{4,20},{20... | collective-permute-start | bytes 1671176 | tf_op jit(solution)/shard_map/ppermute | solution.py:31
  179.8 36.6 %collective-permute-start.69 = (bf16[256,2048]{1,0:T(8,128)(2,1)}, bf16[256,2048]{1,0:T(8,128)(2,1)S(1)}, u32[]{:S(2)}, u32[]{:S(2)}) collective-permute-start(bf16[256,2048]{1,0:T(8,128)(2,1)} %get-tuple-element.614), channel_id=1, source_target_pairs={{0,16},{16,0},{1,17},{17,1},{2,18},{18,2},{3,19},{19,3},{4,20},{20... | collective-permute-start | bytes 3145736 | tf_op jit(solution)/shard_map/ppermute | solution.py:31
  183.2 12.4 %collective-permute-start.63 = (bf16[64,2048]{1,0:T(8,128)(2,1)S(1)}, bf16[64,2048]{1,0:T(8,128)(2,1)S(1)}, u32[]{:S(2)}, u32[]{:S(2)}) collective-permute-start(bf16[64,2048]{1,0:T(8,128)(2,1)S(1)} %get-tuple-element.612.refs_1_), channel_id=1, source_target_pairs={{0,2},{1,3},{2,0},{3,1},{4,6},{5,7},{6,4},{7,5},{8,10},{9,11},{10,... | collective-permute-start | bytes 786440 | tf_op jit(solution)/shard_map/ppermute | solution.py:26
  184.0 13.6 %collective-permute-start.64 = (bf16[64,2048]{1,0:T(8,128)(2,1)S(1)}, bf16[64,2048]{1,0:T(8,128)(2,1)}, u32[]{:S(2)}, u32[]{:S(2)}) collective-permute-start(bf16[64,2048]{1,0:T(8,128)(2,1)S(1)} %get-tuple-element.612.refs_1_), channel_id=1, source_target_pairs={{0,3},{1,2},{2,1},{3,0},{4,7},{5,6},{6,5},{7,4},{8,11},{9,10},{10,... | collective-permute-start | bytes 786440 | tf_op jit(solution)/shard_map/ppermute | solution.py:26
  187.4 10.3 %collective-permute-start.74 = (bf16[272,256]{1,0:T(8,128)(2,1)}, bf16[272,256]{1,0:T(8,128)(2,1)}, u32[]{:S(2)}, u32[]{:S(2)}) collective-permute-start(bf16[272,256]{1,0:T(8,128)(2,1)} %get-tuple-element.620), channel_id=1, source_target_pairs={{12,8},{13,9},{14,10},{15,11},{28,24},{29,25},{30,26},{31,27}} | collective-permute-start | bytes 417800 | tf_op jit(solution)/shard_map/ppermute | solution.py:39
  196.3 16.3 %collective-permute-start.76 = (bf16[272,256]{1,0:T(8,128)(2,1)}, bf16[272,256]{1,0:T(8,128)(2,1)}, u32[]{:S(2)}, u32[]{:S(2)}) collective-permute-start(bf16[272,256]{1,0:T(8,128)(2,1)} %get-tuple-element.622), channel_id=1, source_target_pairs={{12,0},{13,1},{14,2},{15,3},{28,16},{29,17},{30,18},{31,19}} | collective-permute-start | bytes 417800 | tf_op jit(solution)/shard_map/ppermute | solution.py:39
  197.6 18.7 %collective-permute-start.65 = (bf16[64,2048]{1,0:T(8,128)(2,1)S(1)}, bf16[64,2048]{1,0:T(8,128)(2,1)S(1)}, u32[]{:S(2)}, u32[]{:S(2)}) collective-permute-start(bf16[64,2048]{1,0:T(8,128)(2,1)S(1)} %get-tuple-element.612.refs_1_), channel_id=1, source_target_pairs={{0,16},{16,0},{1,17},{17,1},{2,18},{18,2},{3,19},{19,3},{4,20},{20... | collective-permute-start | bytes 786440 | tf_op jit(solution)/shard_map/ppermute | solution.py:31
  197.7 18.6 %collective-permute-start.66 = (bf16[64,2048]{1,0:T(8,128)(2,1)}, bf16[64,2048]{1,0:T(8,128)(2,1)S(1)}, u32[]{:S(2)}, u32[]{:S(2)}) collective-permute-start(bf16[64,2048]{1,0:T(8,128)(2,1)} %copy-done.2), channel_id=1, source_target_pairs={{0,16},{16,0},{1,17},{17,1},{2,18},{18,2},{3,19},{19,3},{4,20},{20... | collective-permute-start | bytes 786440 | tf_op jit(solution)/shard_map/ppermute | solution.py:31
  198.2 18.1 %collective-permute-start.67 = (bf16[64,2048]{1,0:T(8,128)(2,1)}, bf16[64,2048]{1,0:T(8,128)(2,1)S(1)}, u32[]{:S(2)}, u32[]{:S(2)}) collective-permute-start(bf16[64,2048]{1,0:T(8,128)(2,1)} %copy-done.4), channel_id=1, source_target_pairs={{0,16},{16,0},{1,17},{17,1},{2,18},{18,2},{3,19},{19,3},{4,20},{20... | collective-permute-start | bytes 786440 | tf_op jit(solution)/shard_map/ppermute | solution.py:31
  (42 other events, 288.7 us)
where the time goes:
time: 227 us; the launch traced here: 223 us
  waiting for transfers between devices  118 us (52%)
  starting transfers between devices  46.9 us (21%)
  Pallas kernels  36.8 us (16%)
  local copies, waits for them, and re-layouts  10.1 us (4%)
  other arithmetic  5.9 us (3%)
  between operations  5.3 us (2%)
    ppermute x16, waiting for transfers between devices, hop(): return lax.ppermute(value, 'section', [(source, target)])  85.4 us
    pallas_call x30, Pallas kernels, call(): pl.pallas_call(inner, in_specs=list(specs) + [ANY] * waits, compiler_para...  34.4 us
    ppermute x18, waiting for transfers between devices, mp_swap(): return lax.ppermute(value, 'mp', [(m, m ^ flip) for m in range(count)])  31.1 us
    ppermute x18, starting transfers between devices, mp_swap(): return lax.ppermute(value, 'mp', [(m, m ^ flip) for m in range(count)])  22.3 us
    ppermute x16, starting transfers between devices, hop(): return lax.ppermute(value, 'section', [(source, target)])  15.8 us
    unnamed x28, local copies, waits for them, and re-layouts  5.84 us
  transfers between devices with their start and end apart: 60, of which 16 were waited for; matrix products, arithmetic and copies ran while one was open for 4% of the time, Pallas kernels for 12%

commit v1 on v0

--- a/solution.py
+++ b/solution.py
@@ -334,8 +334,9 @@
 def pack_columns(deps, ids, chunks, tails, level, n_dp, n_mp, blk):
     count = len(chunks)
     height, _ = chunks[0].shape
-    tail_rows, tail_width = tails[0].shape if tails else (height, 0)
+    tail_width = tails[0].shape[1] if tails else 0
     core = n_dp * blk
+    end = count * height
 
     def body(ids_ref, *refs):
         chunk_refs, rest = refs[:count], refs[count:]
@@ -344,20 +345,23 @@
         def fill():
             for k, out in enumerate(outs):
                 for c, chunk_ref in enumerate(chunk_refs):
-                    first = c * tail_rows
+                    first = c * height
                     for d in range(n_dp):
                         col = pl.multiple_of((ids_ref[3 + k] + d * n_mp) * blk, blk)
                         out[first : first + height, d * blk : (d + 1) * blk] = chunk_ref[:, pl.ds(col, blk)]
                     if tails:
-                        out[first + height : first + tail_rows, :core] = jnp.zeros((EXTRA, core), BF16)
-                        out[first : first + tail_rows, core:] = tail_refs[c][...]
+                        out[first : first + height, core:] = tail_refs[c][:height, :]
+                if tails:
+                    sums = [ref[height:, :].astype(F32)[: EXTRA // 2] for ref in tail_refs]
+                    out[end:, :core] = jnp.zeros((EXTRA, core), BF16)
+                    out[end:, core:] = jnp.concatenate(sums, axis=0).astype(BF16)
 
         if level is None:
             fill()
         else:
             pl.when(ids_ref[0] == level)(fill)
 
-    shape = jax.ShapeDtypeStruct((count * tail_rows, core + tail_width), BF16)
+    shape = jax.ShapeDtypeStruct((end + (EXTRA if tails else 0), core + tail_width), BF16)
     return call(
         body,
         [ids, *chunks, *tails],
@@ -379,7 +383,7 @@
     return jnp.where(line == 0, high, jnp.where(line == 1, loss - high, 0.0))
 
 
-def head_partial(deps, ids, pieces, level, blk, height):
+def head_partial(deps, ids, pieces, level, blk):
     rows_each, wide = pieces[0].shape
     core = 2 * blk
     out_width = wide - core
@@ -400,8 +404,9 @@
                 copies.append(pltpu.make_async_copy(ref.at[:, core:], right.at[rows], sems.at[2, i]))
             run_copies(copies)
             loss = jnp.zeros((1, 128), F32)
-            for first in range(height, many * rows_each, height + EXTRA):
-                loss = loss + right[first : first + 1, :128].astype(F32) + right[first + 1 : first + 2, :128].astype(F32)
+            for piece in range(1, many + 1):
+                tail = right[piece * rows_each - EXTRA : piece * rows_each, :128].astype(F32)
+                loss = loss + tail[0:1] + tail[1:2] + tail[EXTRA // 2 : EXTRA // 2 + 1] + tail[EXTRA // 2 + 1 : EXTRA // 2 + 2]
             tail = loss_rows(loss[:, :1], out_width)
             part = lax.dot_general(left[...], right[...], (((0,), (0,)), ((), ())), preferred_element_type=F32)
             mine_ref[:blk, :] = part[:blk]
@@ -738,18 +743,16 @@
             sends = pack_columns(token, ids, entered, [], None, n_dp, n_mp, blk)
             token = [sends[0]]
             hidden_pieces = [sends[0]] + [mp_swap(sends[k], k) for k in range(1, n_mp)]
-        elif level == last - 2:
-            hidden_pieces = both_groups(hidden_pieces)
-            token = [*token, *hidden_pieces]
 
     cols = out_width // n_sec
     if small:
         swapped = []
         for c in backward_order:
             swapped.append([mixes[c]] + [mp_swap(mixes[c], k) for k in range(1, n_mp)])
+        hidden_pieces = both_groups(hidden_pieces)
         first_mine, send, turned = first_gradient([], ids, hidden_pieces, swapped[0], blk, height)
         first_other = dp_swap(send)
-        mine, send = head_partial([], ids, head_pieces, last, blk, height)
+        mine, send = head_partial([], ids, head_pieces, last, blk)
         other = dp_swap(send)
         blocks = head_gradient([], ids, mine, other, last, blk, n_sec)
         arrived = [hop(blocks[j], last, j) for j in range(last)]

time: 227 us -> 221 us (0.974); the launches traced: 223 us -> 220 us
  transfers between devices with their start and end apart: 60 -> 60, of which waited for: 16 -> 17; matrix products, arithmetic and copies ran while one was open for 4% -> 4% of each run, Pallas kernels for 12% -> 12%
where the time goes in v1:
time: 221 us; the launch traced here: 220 us
  waiting for transfers between devices  116 us (52%)
  starting transfers between devices  45.8 us (21%)
  Pallas kernels  36.9 us (17%)
  local copies, waits for them, and re-layouts  10.1 us (5%)
  other arithmetic  5.9 us (3%)
  between operations  5.3 us (2%)
    ppermute x16, waiting for transfers between devices, hop(): return lax.ppermute(value, 'section', [(source, target)])  83.7 us
    pallas_call x30, Pallas kernels, call(): pl.pallas_call(inner, in_specs=list(specs) + [ANY] * waits, compiler_para...  34.4 us
    ppermute x18, waiting for transfers between devices, mp_swap(): return lax.ppermute(value, 'mp', [(m, m ^ flip) for m in range(count)])  29.4 us
    ppermute x18, starting transfers between devices, mp_swap(): return lax.ppermute(value, 'mp', [(m, m ^ flip) for m in range(count)])  22 us
    ppermute x16, starting transfers between devices, hop(): return lax.ppermute(value, 'section', [(source, target)])  15.8 us
    unnamed x28, local copies, waits for them, and re-layouts  5.84 us
  transfers between devices with their start and end apart: 60, of which 17 were waited for; matrix products, arithmetic and copies ran while one was open for 4% of the time, Pallas kernels for 12%

profile of v1, /device:TPU:0, one launch (start us, length us, event | category | flops | bytes accessed | tf_op | source)
XLA Modules:
  0.0 219.8 jit_solution(9563126450846144883)
XLA Ops:
  2.4 3.0 %collective-permute-start.17 = (s32[2,6]{1,0:T(2,128)S(1)}, s32[2,6]{1,0:T(2,128)S(1)}, u32[]{:S(2)}, u32[]{:S(2)}) collective-permute-start(s32[2,6]{1,0:T(2,128)S(1)} %get-tuple-element.748), channel_id=1, source_target_pairs={{0,1},{1,0},{2,3},{3,2},{4,5},{5,4},{6,7},{7,6},{8,9},{9,8},{10,11... | collective-permute-start | bytes 152 | tf_op jit(solution)/shard_map/ppermute | solution.py:26
  5.4 1.5 collective-permute-start.18
  6.9 1.6 join.2.refs_2_
  9.3 2.3 %dynamic-slice_bitcast_fusion.6 = (bf16[128,2048]{1,0:T(8,128)(2,1)}, bf16[128,2048]{1,0:T(8,128)(2,1)}) fusion(bf16[1,512,2048]{2,1,0:T(8,128)(2,1)} %param.24, s32[]{:T(128)S(6)} %select_n.205, s32[]{:T(128)S(6)} %select_n.204), kind=kLoop, calls=%fused_computation.55 | loop fusion | bytes 2097160 | tf_op jit(solution)/shard_map/dynamic_slice | solution.py:91
  12.4 2.0 collective-permute-start.21
  14.4 1.5 collective-permute-start.24
  22.7 4.9 %collective-permute-done.21.refs_2_ = bf16[128,2048]{1,0:T(8,128)(2,1)} collective-permute-done((bf16[128,2048]{1,0:T(8,128)(2,1)}, bf16[128,2048]{1,0:T(8,128)(2,1)}, u32[]{:S(2)}, u32[]{:S(2)}) %collective-permute-start.21) | collective-permute-done | bytes 524320 | tf_op jit(solution)/shard_map/ppermute | solution.py:26
  27.6 19.1 %collective-permute-done.36.rows_ref = bf16[128,512]{1,0:T(8,128)(2,1)S(1)} collective-permute-done((bf16[128,512]{1,0:T(8,128)(2,1)S(1)}, bf16[128,512]{1,0:T(8,128)(2,1)S(1)}, u32[]{:S(2)}, u32[]{:S(2)}) %collective-permute-start.36) | collective-permute-done | bytes 131104 | tf_op jit(solution)/shard_map/ppermute | solution.py:39
  46.6 1.5 collective-permute-start.22
  50.4 5.7 %collective-permute-done.22.refs_1_ = bf16[128,2048]{1,0:T(8,128)(2,1)} collective-permute-done((bf16[128,2048]{1,0:T(8,128)(2,1)}, bf16[128,2048]{1,0:T(8,128)(2,1)}, u32[]{:S(2)}, u32[]{:S(2)}) %collective-permute-start.22) | collective-permute-done | bytes 524320 | tf_op jit(solution)/shard_map/ppermute | solution.py:26
  56.1 1.5 collective-permute-done.25.refs_3_
  59.4 2.4 %lift.1 = (bf16[64,2048]{1,0:T(8,128)(2,1)S(1)}, bf16[64,2048]{1,0:T(8,128)(2,1)S(1)}) custom-call(s32[8]{0:T(128)S(1)} %stack.60.refs_0_.ids_ref, bf16[128,512]{1,0:T(8,128)(2,1)S(1)} %collective-permute-done.36.rows_ref, bf16[512,2048]{1,0:T(8,128)(2,1)} %encoder_ref.1), custom_call_target="tpu_custom_call" | custom-call | tf_op jit(solution)/shard_map/lift/pallas_call | solution.py:324
  61.9 2.8 %assemble.1.refs_5_ = bf16[2048,2048]{1,0:T(8,128)(2,1)S(1)} custom-call(s32[8]{0:T(128)S(1)} %stack.60.refs_0_.ids_ref, bf16[512,2048]{1,0:T(8,128)(2,1)S(1)} %bitcast.126, bf16[128,2048]{1,0:T(8,128)(2,1)} %collective-permute-done.21.refs_2_, bf16[128,2048]{1,0:T(8,128)(2,1)} %copy-done.20, bf16[128,2048]{1,0:T(8,128)(2,1)} %collective-permute-done.24.refs_4_, ...), custom_call_target="tpu_custom_call" | custom-call | tf_op jit(solution)/shard_map/assemble/pallas_call | solution.py:59
  64.7 2.1 complete.1.refs_1_.refs_6_.refs_7_
  66.8 3.2 %fwd0.2 = (bf16[64,2048]{1,0:T(8,128)(2,1)S(1)}, bf16[64,2048]{1,0:T(8,128)(2,1)S(1)}, bf16[64,2048]{1,0:T(8,128)(2,1)S(1)}, f32[24,2048]{1,0:T(8,128)S(1)}) custom-call(s32[8]{0:T(128)S(1)} %stack.60.refs_0_.ids_ref, bf16[2048,2048]{1,0:T(8,128)(2,1)S(1)} %complete.1.refs_1_.refs_6_.refs_7_, bf16[64,2048]{1,0:T(8,128)(2,1)S(1)} %get-tuple-element.552.refs_2_, ...), custom_call_target="tpu_custom_call" | custom-call | flops 2147483648 | bytes 8388608 | tf_op jit(solution)/shard_map/fwd0/pallas_call | solution.py:59
  71.3 2.7 %fwd0.3 = (bf16[64,2048]{1,0:T(8,128)(2,1)S(1)}, bf16[64,2048]{1,0:T(8,128)(2,1)S(1)}, bf16[64,2048]{1,0:T(8,128)(2,1)S(1)}) custom-call(s32[8]{0:T(128)S(1)} %stack.60.refs_0_.ids_ref, bf16[2048,2048]{1,0:T(8,128)(2,1)S(1)} %complete.1.refs_1_.refs_6_.refs_7_, bf16[64,2048]{1,0:T(8,128)(2,1)S(1)} %get-tuple-element.555.refs_2_, ...), custom_call_target="tpu_custom_call" | custom-call | flops 2147483648 | bytes 8388608 | tf_op jit(solution)/shard_map/fwd0/pallas_call | solution.py:59
  75.3 2.6 %collective-permute-done.37.refs_2_ = bf16[64,2048]{1,0:T(8,128)(2,1)S(1)} collective-permute-done((bf16[64,2048]{1,0:T(8,128)(2,1)S(1)}, bf16[64,2048]{1,0:T(8,128)(2,1)S(1)}, u32[]{:S(2)}, u32[]{:S(2)}) %collective-permute-start.37) | collective-permute-done | bytes 262176 | tf_op jit(solution)/shard_map/ppermute | solution.py:39
  79.2 4.2 %collective-permute-done.39.refs_2_ = bf16[64,2048]{1,0:T(8,128)(2,1)S(1)} collective-permute-done((bf16[64,2048]{1,0:T(8,128)(2,1)S(1)}, bf16[64,2048]{1,0:T(8,128)(2,1)S(1)}, u32[]{:S(2)}, u32[]{:S(2)}) %collective-permute-start.39) | collective-permute-done | bytes 262176 | tf_op jit(solution)/shard_map/ppermute | solution.py:39
  91.0 1.6 copy-done.9
  101.7 2.4 %collective-permute-start.50 = (bf16[128,512]{1,0:T(8,128)(2,1)S(1)}, bf16[128,512]{1,0:T(8,128)(2,1)S(1)}, u32[]{:S(2)}, u32[]{:S(2)}) collective-permute-start(bf16[128,512]{1,0:T(8,128)(2,1)S(1)} %get-tuple-element.594), channel_id=1, source_target_pairs={{0,3},{1,2},{2,1},{3,0},{4,7},{5,6},{6,5},{7,4},{8,11},{9,10},{10,... | collective-permute-start | bytes 393224 | tf_op jit(solution)/shard_map/ppermute | solution.py:26
  112.0 45.0 %collective-permute-done.56.refs_1_ = bf16[64,2048]{1,0:T(8,128)(2,1)S(1)} collective-permute-done((bf16[64,2048]{1,0:T(8,128)(2,1)S(1)}, bf16[64,2048]{1,0:T(8,128)(2,1)S(1)}, u32[]{:S(2)}, u32[]{:S(2)}) %collective-permute-start.56) | collective-permute-done | bytes 262176 | tf_op jit(solution)/shard_map/ppermute | solution.py:39
  158.3 2.5 %collective-permute-start.58 = (bf16[64,2048]{1,0:T(8,128)(2,1)S(1)}, bf16[64,2048]{1,0:T(8,128)(2,1)S(1)}, u32[]{:S(2)}, u32[]{:S(2)}) collective-permute-start(bf16[64,2048]{1,0:T(8,128)(2,1)S(1)} %get-tuple-element.606.refs_9_), channel_id=1, source_target_pairs={{0,1},{1,0},{2,3},{3,2},{4,5},{5,4},{6,7},{7,6},{8,9},{9,8},{10,11... | collective-permute-start | bytes 786440 | tf_op jit(solution)/shard_map/ppermute | solution.py:26
  160.9 1.5 collective-permute-start.59
  165.3 2.7 %collective-permute-done.58.refs_10_ = bf16[64,2048]{1,0:T(8,128)(2,1)S(1)} collective-permute-done((bf16[64,2048]{1,0:T(8,128)(2,1)S(1)}, bf16[64,2048]{1,0:T(8,128)(2,1)S(1)}, u32[]{:S(2)}, u32[]{:S(2)}) %collective-permute-start.58) | collective-permute-done | bytes 262176 | tf_op jit(solution)/shard_map/ppermute | solution.py:26
  168.0 6.9 %collective-permute-done.59.refs_11_ = bf16[64,2048]{1,0:T(8,128)(2,1)S(1)} collective-permute-done((bf16[64,2048]{1,0:T(8,128)(2,1)S(1)}, bf16[64,2048]{1,0:T(8,128)(2,1)S(1)}, u32[]{:S(2)}, u32[]{:S(2)}) %collective-permute-start.59) | collective-permute-done | bytes 262176 | tf_op jit(solution)/shard_map/ppermute | solution.py:26
  174.9 2.8 %first_gradient.1 = (f32[256,2048]{1,0:T(8,128)S(1)}, bf16[256,2048]{1,0:T(8,128)(2,1)}, bf16[256,512]{1,0:T(8,128)(2,1)S(1)}) custom-call(s32[8]{0:T(128)S(1)} %stack.60.refs_0_.ids_ref, bf16[128,512]{1,0:T(8,128)(2,1)S(1)} %get-tuple-element.591.refs_8_.refs_1_, bf16[128,512]{1,0:T(8,128)(2,1)S(1)} %collective-permute-done.48.refs_2_, ...), custom_call_target="tpu_custom_call" | custom-call | tf_op jit(solution)/shard_map/first_gradient/pallas_call | solution.py:59
  177.8 2.0 bwd0.3
  182.0 1.4 collective-permute-start.64
  186.7 2.4 %collective-permute-done.62.refs_2_ = bf16[64,2048]{1,0:T(8,128)(2,1)S(1)} collective-permute-done((bf16[64,2048]{1,0:T(8,128)(2,1)S(1)}, bf16[64,2048]{1,0:T(8,128)(2,1)S(1)}, u32[]{:S(2)}, u32[]{:S(2)}) %collective-permute-start.62) | collective-permute-done | bytes 262176 | tf_op jit(solution)/shard_map/ppermute | solution.py:26
  190.4 3.1 %collective-permute-done.63.refs_3_ = bf16[64,2048]{1,0:T(8,128)(2,1)S(1)} collective-permute-done((bf16[64,2048]{1,0:T(8,128)(2,1)S(1)}, bf16[64,2048]{1,0:T(8,128)(2,1)S(1)}, u32[]{:S(2)}, u32[]{:S(2)}) %collective-permute-start.63) | collective-permute-done | bytes 262176 | tf_op jit(solution)/shard_map/ppermute | solution.py:26
  196.2 12.8 %collective-permute-done.76 = bf16[272,256]{1,0:T(8,128)(2,1)} collective-permute-done((bf16[272,256]{1,0:T(8,128)(2,1)}, bf16[272,256]{1,0:T(8,128)(2,1)}, u32[]{:S(2)}, u32[]{:S(2)}) %collective-permute-start.76) | collective-permute-done | bytes 139296 | tf_op jit(solution)/shard_map/ppermute | solution.py:39
  215.7 3.0 %last_gradient.1 = f32[256,2048]{1,0:T(8,128)} custom-call(bf16[256,512]{1,0:T(8,128)(2,1)S(1)} %copy-done.1, bf16[64,2048]{1,0:T(8,128)(2,1)S(1)} %get-tuple-element.612.refs_1_, bf16[64,2048]{1,0:T(8,128)(2,1)S(1)} %copy-done.3, bf16[64,2048]{1,0:T(8,128)(2,1)S(1)} %copy-done.5, bf16[64,2048]{1,0:T(8,128)(2,1)} %collective-permute-done.64.refs_4_, ...), custom_call_target="tpu_custom_call" | custom-call | tf_op jit(solution)/shard_map/last_gradient/pallas_call | solution.py:59
  (187 shorter events, 59.6 us)
Async XLA Ops:
  2.4 10.0 %collective-permute-start.17 = (s32[2,6]{1,0:T(2,128)S(1)}, s32[2,6]{1,0:T(2,128)S(1)}, u32[]{:S(2)}, u32[]{:S(2)}) collective-permute-start(s32[2,6]{1,0:T(2,128)S(1)} %get-tuple-element.748), channel_id=1, source_target_pairs={{0,1},{1,0},{2,3},{3,2},{4,5},{5,4},{6,7},{7,6},{8,9},{9,8},{10,11... | collective-permute-start | bytes 152 | tf_op jit(solution)/shard_map/ppermute | solution.py:26
  8.5 10.2 %collective-permute-start.33 = (bf16[208,512]{1,0:T(8,128)(2,1)S(1)}, bf16[208,512]{1,0:T(8,128)(2,1)S(1)}, u32[]{:S(2)}, u32[]{:S(2)}) collective-permute-start(bf16[208,512]{1,0:T(8,128)(2,1)S(1)} %join.2.refs_2_), channel_id=1, source_target_pairs={{12,13},{13,12},{14,15},{15,14},{28,29},{29,28},{30,31},{31,30}} | collective-permute-start | bytes 638984 | tf_op jit(solution)/shard_map/ppermute | solution.py:46
  12.4 15.2 %collective-permute-start.21 = (bf16[128,2048]{1,0:T(8,128)(2,1)}, bf16[128,2048]{1,0:T(8,128)(2,1)}, u32[]{:S(2)}, u32[]{:S(2)}) collective-permute-start(bf16[128,2048]{1,0:T(8,128)(2,1)} %get-tuple-element.742), channel_id=1, source_target_pairs={{0,1},{1,0},{2,3},{3,2},{4,5},{5,4},{6,7},{7,6},{8,9},{9,8},{10,11... | collective-permute-start | bytes 1572872 | tf_op jit(solution)/shard_map/ppermute | solution.py:26
  14.4 33.8 %collective-permute-start.24 = (bf16[128,2048]{1,0:T(8,128)(2,1)}, bf16[128,2048]{1,0:T(8,128)(2,1)}, u32[]{:S(2)}, u32[]{:S(2)}) collective-permute-start(bf16[128,2048]{1,0:T(8,128)(2,1)} %get-tuple-element.741), channel_id=1, source_target_pairs={{0,2},{1,3},{2,0},{3,1},{4,6},{5,7},{6,4},{7,5},{8,10},{9,11},{10,... | collective-permute-start | bytes 1572872 | tf_op jit(solution)/shard_map/ppermute | solution.py:26
  18.8 30.9 %collective-permute-start.29 = (bf16[128,2048]{1,0:T(8,128)(2,1)}, bf16[128,2048]{1,0:T(8,128)(2,1)}, u32[]{:S(2)}, u32[]{:S(2)}) collective-permute-start(bf16[128,2048]{1,0:T(8,128)(2,1)} %get-tuple-element.741), channel_id=1, source_target_pairs={{0,1},{1,0},{2,3},{3,2},{4,5},{5,4},{6,7},{7,6},{8,9},{9,8},{10,11... | collective-permute-start | bytes 1572872 | tf_op jit(solution)/shard_map/ppermute | solution.py:26
  19.9 26.7 %collective-permute-start.36 = (bf16[128,512]{1,0:T(8,128)(2,1)S(1)}, bf16[128,512]{1,0:T(8,128)(2,1)S(1)}, u32[]{:S(2)}, u32[]{:S(2)}) collective-permute-start(bf16[128,512]{1,0:T(8,128)(2,1)S(1)} %pick.2), channel_id=1, source_target_pairs={{12,0},{13,1},{14,2},{15,3},{28,16},{29,17},{30,18},{31,19}} | collective-permute-start | bytes 393224 | tf_op jit(solution)/shard_map/ppermute | solution.py:39
  22.6 27.2 %collective-permute-start.31 = (bf16[128,2048]{1,0:T(8,128)(2,1)}, bf16[128,2048]{1,0:T(8,128)(2,1)S(1)}, u32[]{:S(2)}, u32[]{:S(2)}) collective-permute-start(bf16[128,2048]{1,0:T(8,128)(2,1)} %get-tuple-element.742), channel_id=1, source_target_pairs={{0,2},{1,3},{2,0},{3,1},{4,6},{5,7},{6,4},{7,5},{8,10},{9,11},{10,... | collective-permute-start | bytes 1572872 | tf_op jit(solution)/shard_map/ppermute | solution.py:26
  27.6 22.7 %collective-permute-start.27 = (bf16[128,2048]{1,0:T(8,128)(2,1)}, bf16[128,2048]{1,0:T(8,128)(2,1)S(1)}, u32[]{:S(2)}, u32[]{:S(2)}) collective-permute-start(bf16[128,2048]{1,0:T(8,128)(2,1)} %collective-permute-done.21.refs_2_), channel_id=1, source_target_pairs={{0,16},{16,0},{1,17},{17,1},{2,18},{18,2},{3,19},{19,3},{4,20},{20... | collective-permute-start | bytes 1572872 | tf_op jit(solution)/shard_map/ppermute | solution.py:31
  46.6 9.5 %collective-permute-start.22 = (bf16[128,2048]{1,0:T(8,128)(2,1)}, bf16[128,2048]{1,0:T(8,128)(2,1)}, u32[]{:S(2)}, u32[]{:S(2)}) collective-permute-start(bf16[128,2048]{1,0:T(8,128)(2,1)} %collective-permute-done.21.refs_2_), channel_id=1, source_target_pairs={{0,2},{1,3},{2,0},{3,1},{4,6},{5,7},{6,4},{7,5},{8,10},{9,11},{10,... | collective-permute-start | bytes 1572872 | tf_op jit(solution)/shard_map/ppermute | solution.py:26
  48.2 9.5 %collective-permute-start.25 = (bf16[128,2048]{1,0:T(8,128)(2,1)}, bf16[128,2048]{1,0:T(8,128)(2,1)}, u32[]{:S(2)}, u32[]{:S(2)}) collective-permute-start(bf16[128,2048]{1,0:T(8,128)(2,1)} %collective-permute-done.24.refs_4_), channel_id=1, source_target_pairs={{0,1},{1,0},{2,3},{3,2},{4,5},{5,4},{6,7},{7,6},{8,9},{9,8},{10,11... | collective-permute-start | bytes 1572872 | tf_op jit(solution)/shard_map/ppermute | solution.py:26
  49.7 12.1 %collective-permute-start.28 = (bf16[128,2048]{1,0:T(8,128)(2,1)}, bf16[128,2048]{1,0:T(8,128)(2,1)}, u32[]{:S(2)}, u32[]{:S(2)}) collective-permute-start(bf16[128,2048]{1,0:T(8,128)(2,1)} %collective-permute-done.24.refs_4_), channel_id=1, source_target_pairs={{0,16},{16,0},{1,17},{17,1},{2,18},{18,2},{3,19},{19,3},{4,20},{20... | collective-permute-start | bytes 1572872 | tf_op jit(solution)/shard_map/ppermute | solution.py:31
  49.8 12.0 %collective-permute-start.30 = (bf16[128,2048]{1,0:T(8,128)(2,1)}, bf16[128,2048]{1,0:T(8,128)(2,1)}, u32[]{:S(2)}, u32[]{:S(2)}) collective-permute-start(bf16[128,2048]{1,0:T(8,128)(2,1)} %collective-permute-done.29.refs_6_), channel_id=1, source_target_pairs={{0,16},{16,0},{1,17},{17,1},{2,18},{18,2},{3,19},{19,3},{4,20},{20... | collective-permute-start | bytes 1572872 | tf_op jit(solution)/shard_map/ppermute | solution.py:31
  50.3 11.5 %collective-permute-start.32 = (bf16[128,2048]{1,0:T(8,128)(2,1)S(1)}, bf16[128,2048]{1,0:T(8,128)(2,1)}, u32[]{:S(2)}, u32[]{:S(2)}) collective-permute-start(bf16[128,2048]{1,0:T(8,128)(2,1)S(1)} %collective-permute-done.31.refs_8_), channel_id=1, source_target_pairs={{0,16},{16,0},{1,17},{17,1},{2,18},{18,2},{3,19},{19,3},{4,20},{20... | collective-permute-start | bytes 1572872 | tf_op jit(solution)/shard_map/ppermute | solution.py:31
  99.3 11.2 %collective-permute-start.57 = (bf16[64,2048]{1,0:T(8,128)(2,1)S(1)}, bf16[64,2048]{1,0:T(8,128)(2,1)S(1)}, u32[]{:S(2)}, u32[]{:S(2)}) collective-permute-start(bf16[64,2048]{1,0:T(8,128)(2,1)S(1)} %get-tuple-element.601), channel_id=1, source_target_pairs={{8,4},{9,5},{10,6},{11,7},{24,20},{25,21},{26,22},{27,23}} | collective-permute-start | bytes 786440 | tf_op jit(solution)/shard_map/ppermute | solution.py:39
  105.0 52.0 %collective-permute-start.56 = (bf16[64,2048]{1,0:T(8,128)(2,1)S(1)}, bf16[64,2048]{1,0:T(8,128)(2,1)S(1)}, u32[]{:S(2)}, u32[]{:S(2)}) collective-permute-start(bf16[64,2048]{1,0:T(8,128)(2,1)S(1)} %get-tuple-element.598), channel_id=1, source_target_pairs={{4,0},{5,1},{6,2},{7,3},{20,16},{21,17},{22,18},{23,19}} | collective-permute-start | bytes 786440 | tf_op jit(solution)/shard_map/ppermute | solution.py:39
  107.0 51.3 %collective-permute-start.70 = (bf16[144,1536]{1,0:T(8,128)(2,1)S(1)}, bf16[144,1536]{1,0:T(8,128)(2,1)S(1)}, u32[]{:S(2)}, u32[]{:S(2)}) collective-permute-start(bf16[144,1536]{1,0:T(8,128)(2,1)S(1)} %get-tuple-element.615), channel_id=1, source_target_pairs={{12,13},{13,12},{14,15},{15,14},{28,29},{29,28},{30,31},{31,30}} | collective-permute-start | bytes 1327112 | tf_op jit(solution)/shard_map/ppermute | solution.py:739
  109.0 51.8 %collective-permute-start.71 = (bf16[144,1536]{1,0:T(8,128)(2,1)S(1)}, bf16[144,1536]{1,0:T(8,128)(2,1)S(1)}, u32[]{:S(2)}, u32[]{:S(2)}) collective-permute-start(bf16[144,1536]{1,0:T(8,128)(2,1)S(1)} %get-tuple-element.616), channel_id=1, source_target_pairs={{12,14},{13,15},{14,12},{15,13},{28,30},{29,31},{30,28},{31,29}} | collective-permute-start | bytes 1327112 | tf_op jit(solution)/shard_map/ppermute | solution.py:739
  109.7 52.7 %collective-permute-start.72 = (bf16[144,1536]{1,0:T(8,128)(2,1)S(1)}, bf16[144,1536]{1,0:T(8,128)(2,1)S(1)}, u32[]{:S(2)}, u32[]{:S(2)}) collective-permute-start(bf16[144,1536]{1,0:T(8,128)(2,1)S(1)} %get-tuple-element.617), channel_id=1, source_target_pairs={{12,15},{13,14},{14,13},{15,12},{28,31},{29,30},{30,29},{31,28}} | collective-permute-start | bytes 1327112 | tf_op jit(solution)/shard_map/ppermute | solution.py:739
  111.8 50.6 %collective-permute-start.52 = (bf16[128,512]{1,0:T(8,128)(2,1)S(1)}, bf16[128,512]{1,0:T(8,128)(2,1)S(1)}, u32[]{:S(2)}, u32[]{:S(2)}) collective-permute-start(bf16[128,512]{1,0:T(8,128)(2,1)S(1)} %collective-permute-done.48.refs_2_), channel_id=1, source_target_pairs={{0,16},{16,0},{1,17},{17,1},{2,18},{18,2},{3,19},{19,3},{4,20},{20... | collective-permute-start | bytes 393224 | tf_op jit(solution)/shard_map/ppermute | solution.py:31
  158.3 9.7 %collective-permute-start.58 = (bf16[64,2048]{1,0:T(8,128)(2,1)S(1)}, bf16[64,2048]{1,0:T(8,128)(2,1)S(1)}, u32[]{:S(2)}, u32[]{:S(2)}) collective-permute-start(bf16[64,2048]{1,0:T(8,128)(2,1)S(1)} %get-tuple-element.606.refs_9_), channel_id=1, source_target_pairs={{0,1},{1,0},{2,3},{3,2},{4,5},{5,4},{6,7},{7,6},{8,9},{9,8},{10,11... | collective-permute-start | bytes 786440 | tf_op jit(solution)/shard_map/ppermute | solution.py:26
  160.9 14.1 %collective-permute-start.59 = (bf16[64,2048]{1,0:T(8,128)(2,1)S(1)}, bf16[64,2048]{1,0:T(8,128)(2,1)S(1)}, u32[]{:S(2)}, u32[]{:S(2)}) collective-permute-start(bf16[64,2048]{1,0:T(8,128)(2,1)S(1)} %get-tuple-element.606.refs_9_), channel_id=1, source_target_pairs={{0,2},{1,3},{2,0},{3,1},{4,6},{5,7},{6,4},{7,5},{8,10},{9,11},{10,... | collective-permute-start | bytes 786440 | tf_op jit(solution)/shard_map/ppermute | solution.py:26
  162.4 12.5 %collective-permute-start.60 = (bf16[64,2048]{1,0:T(8,128)(2,1)S(1)}, bf16[64,2048]{1,0:T(8,128)(2,1)S(1)}, u32[]{:S(2)}, u32[]{:S(2)}) collective-permute-start(bf16[64,2048]{1,0:T(8,128)(2,1)S(1)} %get-tuple-element.606.refs_9_), channel_id=1, source_target_pairs={{0,3},{1,2},{2,1},{3,0},{4,7},{5,6},{6,5},{7,4},{8,11},{9,10},{10,... | collective-permute-start | bytes 786440 | tf_op jit(solution)/shard_map/ppermute | solution.py:26
  162.4 15.4 %collective-permute-start.61 = (bf16[64,2048]{1,0:T(8,128)(2,1)S(1)}, bf16[64,2048]{1,0:T(8,128)(2,1)S(1)}, u32[]{:S(2)}, u32[]{:S(2)}) collective-permute-start(bf16[64,2048]{1,0:T(8,128)(2,1)S(1)} %get-tuple-element.608), channel_id=1, source_target_pairs={{4,0},{5,1},{6,2},{7,3},{20,16},{21,17},{22,18},{23,19}} | collective-permute-start | bytes 786440 | tf_op jit(solution)/shard_map/ppermute | solution.py:39
  165.1 18.3 %collective-permute-start.73 = (bf16[272,1024]{1,0:T(8,128)(2,1)S(1)}, bf16[272,1024]{1,0:T(8,128)(2,1)S(1)}, u32[]{:S(2)}, u32[]{:S(2)}) collective-permute-start(bf16[272,1024]{1,0:T(8,128)(2,1)S(1)} %get-tuple-element.619), channel_id=1, source_target_pairs={{0,16},{16,0},{1,17},{17,1},{2,18},{18,2},{3,19},{19,3},{4,20},{20... | collective-permute-start | bytes 1671176 | tf_op jit(solution)/shard_map/ppermute | solution.py:31
  177.7 35.1 %collective-permute-start.69 = (bf16[256,2048]{1,0:T(8,128)(2,1)}, bf16[256,2048]{1,0:T(8,128)(2,1)S(1)}, u32[]{:S(2)}, u32[]{:S(2)}) collective-permute-start(bf16[256,2048]{1,0:T(8,128)(2,1)} %get-tuple-element.614), channel_id=1, source_target_pairs={{0,16},{16,0},{1,17},{17,1},{2,18},{18,2},{3,19},{19,3},{4,20},{20... | collective-permute-start | bytes 3145736 | tf_op jit(solution)/shard_map/ppermute | solution.py:31
  181.1 12.4 %collective-permute-start.63 = (bf16[64,2048]{1,0:T(8,128)(2,1)S(1)}, bf16[64,2048]{1,0:T(8,128)(2,1)S(1)}, u32[]{:S(2)}, u32[]{:S(2)}) collective-permute-start(bf16[64,2048]{1,0:T(8,128)(2,1)S(1)} %get-tuple-element.612.refs_1_), channel_id=1, source_target_pairs={{0,2},{1,3},{2,0},{3,1},{4,6},{5,7},{6,4},{7,5},{8,10},{9,11},{10,... | collective-permute-start | bytes 786440 | tf_op jit(solution)/shard_map/ppermute | solution.py:26
  182.0 13.6 %collective-permute-start.64 = (bf16[64,2048]{1,0:T(8,128)(2,1)S(1)}, bf16[64,2048]{1,0:T(8,128)(2,1)}, u32[]{:S(2)}, u32[]{:S(2)}) collective-permute-start(bf16[64,2048]{1,0:T(8,128)(2,1)S(1)} %get-tuple-element.612.refs_1_), channel_id=1, source_target_pairs={{0,3},{1,2},{2,1},{3,0},{4,7},{5,6},{6,5},{7,4},{8,11},{9,10},{10,... | collective-permute-start | bytes 786440 | tf_op jit(solution)/shard_map/ppermute | solution.py:26
  185.4 10.3 %collective-permute-start.74 = (bf16[272,256]{1,0:T(8,128)(2,1)}, bf16[272,256]{1,0:T(8,128)(2,1)}, u32[]{:S(2)}, u32[]{:S(2)}) collective-permute-start(bf16[272,256]{1,0:T(8,128)(2,1)} %get-tuple-element.620), channel_id=1, source_target_pairs={{12,8},{13,9},{14,10},{15,11},{28,24},{29,25},{30,26},{31,27}} | collective-permute-start | bytes 417800 | tf_op jit(solution)/shard_map/ppermute | solution.py:39
  194.2 14.8 %collective-permute-start.76 = (bf16[272,256]{1,0:T(8,128)(2,1)}, bf16[272,256]{1,0:T(8,128)(2,1)}, u32[]{:S(2)}, u32[]{:S(2)}) collective-permute-start(bf16[272,256]{1,0:T(8,128)(2,1)} %get-tuple-element.622), channel_id=1, source_target_pairs={{12,0},{13,1},{14,2},{15,3},{28,16},{29,17},{30,18},{31,19}} | collective-permute-start | bytes 417800 | tf_op jit(solution)/shard_map/ppermute | solution.py:39
  195.5 17.2 %collective-permute-start.65 = (bf16[64,2048]{1,0:T(8,128)(2,1)S(1)}, bf16[64,2048]{1,0:T(8,128)(2,1)S(1)}, u32[]{:S(2)}, u32[]{:S(2)}) collective-permute-start(bf16[64,2048]{1,0:T(8,128)(2,1)S(1)} %get-tuple-element.612.refs_1_), channel_id=1, source_target_pairs={{0,16},{16,0},{1,17},{17,1},{2,18},{18,2},{3,19},{19,3},{4,20},{20... | collective-permute-start | bytes 786440 | tf_op jit(solution)/shard_map/ppermute | solution.py:31
  195.6 17.1 %collective-permute-start.66 = (bf16[64,2048]{1,0:T(8,128)(2,1)}, bf16[64,2048]{1,0:T(8,128)(2,1)S(1)}, u32[]{:S(2)}, u32[]{:S(2)}) collective-permute-start(bf16[64,2048]{1,0:T(8,128)(2,1)} %copy-done.2), channel_id=1, source_target_pairs={{0,16},{16,0},{1,17},{17,1},{2,18},{18,2},{3,19},{19,3},{4,20},{20... | collective-permute-start | bytes 786440 | tf_op jit(solution)/shard_map/ppermute | solution.py:31
  196.1 16.7 %collective-permute-start.67 = (bf16[64,2048]{1,0:T(8,128)(2,1)}, bf16[64,2048]{1,0:T(8,128)(2,1)S(1)}, u32[]{:S(2)}, u32[]{:S(2)}) collective-permute-start(bf16[64,2048]{1,0:T(8,128)(2,1)} %copy-done.4), channel_id=1, source_target_pairs={{0,16},{16,0},{1,17},{17,1},{2,18},{18,2},{3,19},{19,3},{4,20},{20... | collective-permute-start | bytes 786440 | tf_op jit(solution)/shard_map/ppermute | solution.py:31
  (42 other events, 295.5 us)

commit v2 on v1

--- a/solution.py
+++ b/solution.py
@@ -506,25 +506,41 @@
     )
 
 
-def last_gradient(deps, turned, mixes, mine, other):
+def last_gradient(deps, ids, turned, mixes, mine, other, blocks, scale):
     blk, width = mine.shape
     nb = width // BLOCKS
-
-    def body(turned_ref, *refs):
-        mix_refs, (mine_ref, other_ref, out) = refs[:-3], refs[-3:]
+    many = len(mixes)
+    cols = blocks[0].shape[1]
+
+    def body(ids_ref, turned_ref, *refs):
+        mix_refs, (mine_ref, other_ref, *rest) = refs[:many], refs[many:]
+        block_refs, (out, head_out, loss_out) = rest[:-3], rest[-3:]
+        for j, ref in enumerate(block_refs):
+
+            @pl.when(ids_ref[0] == j)
+            def _():
+                head_out[...] = ref[:blk, :].astype(F32)
+                tail = ref[blk:, :].astype(F32)
+                loss_out[...] = (tail[0:1, :128] + tail[1:2, :128]) * scale
+
         for n in range(BLOCKS):
-            cols = slice(n * nb, (n + 1) * nb)
-            right = jnp.concatenate([ref[:, cols] for ref in mix_refs], axis=0)
+            span = slice(n * nb, (n + 1) * nb)
+            right = jnp.concatenate([ref[:, span] for ref in mix_refs], axis=0)
             part = jnp.dot(turned_ref[...], right, preferred_element_type=F32)
-            out[:, cols] = part + mine_ref[:, cols] + other_ref[:, cols].astype(F32)
-
+            out[:, span] = part + mine_ref[:, span] + other_ref[:, span].astype(F32)
+
+    args = [ids, turned, *mixes, mine, other, *blocks]
     return call(
         body,
-        [turned, *mixes, mine, other],
-        [VMEM] * (3 + len(mixes)),
+        args,
+        [SMEM] + [VMEM] * (len(args) - 1),
         deps,
-        out_shape=jax.ShapeDtypeStruct((blk, width), F32),
-        out_specs=VMEM,
+        out_shape=[
+            jax.ShapeDtypeStruct((blk, width), F32),
+            jax.ShapeDtypeStruct((blk, cols), F32),
+            jax.ShapeDtypeStruct((1, 128), F32),
+        ],
+        out_specs=[VMEM] * 3,
         name="last_gradient",
     )
 
@@ -756,12 +772,11 @@
         other = dp_swap(send)
         blocks = head_gradient([], ids, mine, other, last, blk, n_sec)
         arrived = [hop(blocks[j], last, j) for j in range(last)]
-        head_ext = blocks[last].astype(F32)
-        for j in range(last):
-            head_ext = jnp.where(sec == j, arrived[j].astype(F32), head_ext)
-        head_mine = head_ext[:blk]
-        loss_mine = (head_ext[blk, 0] + head_ext[blk + 1, 0]) / (n_dp * MB * out_width)
-        grad = last_gradient([], turned, both_groups(swapped[1]), first_mine, first_other)
+        grad, head_mine, loss_mine = last_gradient(
+            [], ids, turned, both_groups(swapped[1]), first_mine, first_other, [*arrived, blocks[last]],
+            1.0 / (n_dp * MB * out_width),
+        )
+        loss_mine = loss_mine[0, 0]
     else:
         contract = (((0,), (0,)), ((), ()))
         joined = jnp.concatenate(entered, axis=0)

time: 221 us -> 214 us (0.968); the launches traced: 220 us -> 210 us
  local copies, waits for them, and re-layouts: 10.1 us -> 3.68 us
  waiting for transfers between devices: 116 us -> 119 us
  between operations: 5.3 us -> 2.91 us
    ppermute x18, waiting for transfers between devices: 29.4 us -> 35.6 us  [mp_swap(): return lax.ppermute(value, 'mp', [(m, m ^ flip) for m in range(count)])]
    unnamed x28 -> x10, local copies, waits for them, and re-layouts: 5.84 us -> 1.64 us
    ppermute x16, waiting for transfers between devices: 83.7 us -> 80.8 us  [hop(): return lax.ppermute(value, 'section', [(source, target)])]
  transfers between devices with their start and end apart: 60 -> 60, of which waited for: 17 -> 19; matrix products, arithmetic and copies ran while one was open for 4% -> 2% of each run, Pallas kernels for 12% -> 12%
where the time goes in v2:
time: 214 us; the launch traced here: 210 us
  waiting for transfers between devices  119 us (56%)
  starting transfers between devices  43.6 us (20%)
  Pallas kernels  35.6 us (17%)
  other arithmetic  4.58 us (2%)
  local copies, waits for them, and re-layouts  3.68 us (2%)
  between operations  2.91 us (1%)
    ppermute x16, waiting for transfers between devices, hop(): return lax.ppermute(value, 'section', [(source, target)])  80.8 us
    ppermute x18, waiting for transfers between devices, mp_swap(): return lax.ppermute(value, 'mp', [(m, m ^ flip) for m in range(count)])  35.6 us
    pallas_call x30, Pallas kernels, call(): pl.pallas_call(inner, in_specs=list(specs) + [ANY] * waits, compiler_para...  33.1 us
    ppermute x18, starting transfers between devices, mp_swap(): return lax.ppermute(value, 'mp', [(m, m ^ flip) for m in range(count)])  20.7 us
    ppermute x16, starting transfers between devices, hop(): return lax.ppermute(value, 'section', [(source, target)])  14.5 us
  transfers between devices with their start and end apart: 60, of which 19 were waited for; matrix products, arithmetic and copies ran while one was open for 2% of the time, Pallas kernels for 12%

profile of v2, /device:TPU:0, one launch (start us, length us, event | category | flops | bytes accessed | tf_op | source)
XLA Modules:
  0.0 210.0 jit_solution(12806261566455660594)
XLA Ops:
  2.2 3.0 %collective-permute-start.17 = (s32[2,6]{1,0:T(2,128)S(1)}, s32[2,6]{1,0:T(2,128)S(1)}, u32[]{:S(2)}, u32[]{:S(2)}) collective-permute-start(s32[2,6]{1,0:T(2,128)S(1)} %get-tuple-element.752), channel_id=1, source_target_pairs={{0,1},{1,0},{2,3},{3,2},{4,5},{5,4},{6,7},{7,6},{8,9},{9,8},{10,11... | collective-permute-start | bytes 152 | tf_op jit(solution)/shard_map/ppermute | solution.py:26
  5.2 1.5 collective-permute-start.18
  6.8 1.6 join.2.refs_2_
  11.3 2.0 collective-permute-start.21
  13.3 1.5 collective-permute-start.24
  21.5 4.7 %collective-permute-done.21.refs_2_ = bf16[128,2048]{1,0:T(8,128)(2,1)} collective-permute-done((bf16[128,2048]{1,0:T(8,128)(2,1)S(1)}, bf16[128,2048]{1,0:T(8,128)(2,1)}, u32[]{:S(2)}, u32[]{:S(2)}) %collective-permute-start.21) | collective-permute-done | bytes 524320 | tf_op jit(solution)/shard_map/ppermute | solution.py:26
  26.2 19.1 %collective-permute-done.36.rows_ref = bf16[128,512]{1,0:T(8,128)(2,1)S(1)} collective-permute-done((bf16[128,512]{1,0:T(8,128)(2,1)S(1)}, bf16[128,512]{1,0:T(8,128)(2,1)S(1)}, u32[]{:S(2)}, u32[]{:S(2)}) %collective-permute-start.36) | collective-permute-done | bytes 131104 | tf_op jit(solution)/shard_map/ppermute | solution.py:39
  45.3 1.5 collective-permute-start.22
  49.1 5.7 %collective-permute-done.22.refs_1_ = bf16[128,2048]{1,0:T(8,128)(2,1)} collective-permute-done((bf16[128,2048]{1,0:T(8,128)(2,1)}, bf16[128,2048]{1,0:T(8,128)(2,1)}, u32[]{:S(2)}, u32[]{:S(2)}) %collective-permute-start.22) | collective-permute-done | bytes 524320 | tf_op jit(solution)/shard_map/ppermute | solution.py:26
  54.8 1.5 collective-permute-done.25.refs_3_
  58.0 2.4 %lift.1 = (bf16[64,2048]{1,0:T(8,128)(2,1)S(1)}, bf16[64,2048]{1,0:T(8,128)(2,1)S(1)}) custom-call(s32[8]{0:T(128)S(1)} %stack.60.refs_0_.ids_ref, bf16[128,512]{1,0:T(8,128)(2,1)S(1)} %collective-permute-done.36.rows_ref, bf16[512,2048]{1,0:T(8,128)(2,1)} %encoder_ref.1), custom_call_target="tpu_custom_call" | custom-call | tf_op jit(solution)/shard_map/lift/pallas_call | solution.py:324
  60.4 3.4 %assemble.1.refs_5_ = bf16[2048,2048]{1,0:T(8,128)(2,1)S(1)} custom-call(s32[8]{0:T(128)S(1)} %stack.60.refs_0_.ids_ref, bf16[512,2048]{1,0:T(8,128)(2,1)} %bitcast.42.refs_1_, bf16[128,2048]{1,0:T(8,128)(2,1)} %collective-permute-done.21.refs_2_, bf16[128,2048]{1,0:T(8,128)(2,1)} %collective-permute-done.27.refs_3_, ...), custom_call_target="tpu_custom_call" | custom-call | tf_op jit(solution)/shard_map/assemble/pallas_call | solution.py:59
  63.9 2.1 complete.1.refs_1_.refs_6_.refs_7_
  66.0 3.2 %fwd0.2 = (bf16[64,2048]{1,0:T(8,128)(2,1)S(1)}, bf16[64,2048]{1,0:T(8,128)(2,1)S(1)}, bf16[64,2048]{1,0:T(8,128)(2,1)S(1)}, f32[24,2048]{1,0:T(8,128)S(1)}) custom-call(s32[8]{0:T(128)S(1)} %stack.60.refs_0_.ids_ref, bf16[2048,2048]{1,0:T(8,128)(2,1)S(1)} %complete.1.refs_1_.refs_6_.refs_7_, bf16[64,2048]{1,0:T(8,128)(2,1)S(1)} %get-tuple-element.555.refs_2_, ...), custom_call_target="tpu_custom_call" | custom-call | flops 2147483648 | bytes 8388608 | tf_op jit(solution)/shard_map/fwd0/pallas_call | solution.py:59
  70.5 2.7 %fwd0.3 = (bf16[64,2048]{1,0:T(8,128)(2,1)S(1)}, bf16[64,2048]{1,0:T(8,128)(2,1)S(1)}, bf16[64,2048]{1,0:T(8,128)(2,1)S(1)}) custom-call(s32[8]{0:T(128)S(1)} %stack.60.refs_0_.ids_ref, bf16[2048,2048]{1,0:T(8,128)(2,1)S(1)} %complete.1.refs_1_.refs_6_.refs_7_, bf16[64,2048]{1,0:T(8,128)(2,1)S(1)} %get-tuple-element.558.refs_2_, ...), custom_call_target="tpu_custom_call" | custom-call | flops 2147483648 | bytes 8388608 | tf_op jit(solution)/shard_map/fwd0/pallas_call | solution.py:59
  74.5 2.6 %collective-permute-done.37.refs_2_ = bf16[64,2048]{1,0:T(8,128)(2,1)S(1)} collective-permute-done((bf16[64,2048]{1,0:T(8,128)(2,1)S(1)}, bf16[64,2048]{1,0:T(8,128)(2,1)S(1)}, u32[]{:S(2)}, u32[]{:S(2)}) %collective-permute-start.37) | collective-permute-done | bytes 262176 | tf_op jit(solution)/shard_map/ppermute | solution.py:39
  78.4 4.2 %collective-permute-done.39.refs_2_ = bf16[64,2048]{1,0:T(8,128)(2,1)S(1)} collective-permute-done((bf16[64,2048]{1,0:T(8,128)(2,1)S(1)}, bf16[64,2048]{1,0:T(8,128)(2,1)S(1)}, u32[]{:S(2)}, u32[]{:S(2)}) %collective-permute-start.39) | collective-permute-done | bytes 262176 | tf_op jit(solution)/shard_map/ppermute | solution.py:39
  90.7 1.6 copy-done.4
  104.2 1.4 collective-permute-done.48.refs_2_
  108.7 4.3 %collective-permute-done.50.refs_4_ = bf16[128,512]{1,0:T(8,128)(2,1)S(1)} collective-permute-done((bf16[128,512]{1,0:T(8,128)(2,1)S(1)}, bf16[128,512]{1,0:T(8,128)(2,1)S(1)}, u32[]{:S(2)}, u32[]{:S(2)}) %collective-permute-start.50) | collective-permute-done | bytes 131104 | tf_op jit(solution)/shard_map/ppermute | solution.py:26
  113.0 43.1 %collective-permute-done.56.refs_1_ = bf16[64,2048]{1,0:T(8,128)(2,1)S(1)} collective-permute-done((bf16[64,2048]{1,0:T(8,128)(2,1)S(1)}, bf16[64,2048]{1,0:T(8,128)(2,1)S(1)}, u32[]{:S(2)}, u32[]{:S(2)}) %collective-permute-start.56) | collective-permute-done | bytes 262176 | tf_op jit(solution)/shard_map/ppermute | solution.py:39
  157.5 2.5 %collective-permute-start.58 = (bf16[64,2048]{1,0:T(8,128)(2,1)S(1)}, bf16[64,2048]{1,0:T(8,128)(2,1)S(1)}, u32[]{:S(2)}, u32[]{:S(2)}) collective-permute-start(bf16[64,2048]{1,0:T(8,128)(2,1)S(1)} %get-tuple-element.609.refs_9_), channel_id=1, source_target_pairs={{0,1},{1,0},{2,3},{3,2},{4,5},{5,4},{6,7},{7,6},{8,9},{9,8},{10,11... | collective-permute-start | bytes 786440 | tf_op jit(solution)/shard_map/ppermute | solution.py:26
  160.0 1.5 collective-permute-start.59
  165.1 2.0 collective-permute-done.58.refs_10_
  167.1 6.9 %collective-permute-done.59.refs_11_ = bf16[64,2048]{1,0:T(8,128)(2,1)S(1)} collective-permute-done((bf16[64,2048]{1,0:T(8,128)(2,1)S(1)}, bf16[64,2048]{1,0:T(8,128)(2,1)S(1)}, u32[]{:S(2)}, u32[]{:S(2)}) %collective-permute-start.59) | collective-permute-done | bytes 262176 | tf_op jit(solution)/shard_map/ppermute | solution.py:26
  174.0 1.8 first_gradient.1
  176.2 2.0 bwd0.3
  180.3 1.5 collective-permute-start.64
  182.4 5.1 %collective-permute-done.62.refs_3_ = bf16[64,2048]{1,0:T(8,128)(2,1)S(1)} collective-permute-done((bf16[64,2048]{1,0:T(8,128)(2,1)S(1)}, bf16[64,2048]{1,0:T(8,128)(2,1)S(1)}, u32[]{:S(2)}, u32[]{:S(2)}) %collective-permute-start.62) | collective-permute-done | bytes 262176 | tf_op jit(solution)/shard_map/ppermute | solution.py:26
  188.8 2.9 %collective-permute-done.63.refs_4_ = bf16[64,2048]{1,0:T(8,128)(2,1)S(1)} collective-permute-done((bf16[64,2048]{1,0:T(8,128)(2,1)S(1)}, bf16[64,2048]{1,0:T(8,128)(2,1)S(1)}, u32[]{:S(2)}, u32[]{:S(2)}) %collective-permute-start.63) | collective-permute-done | bytes 262176 | tf_op jit(solution)/shard_map/ppermute | solution.py:26
  193.9 11.5 %collective-permute-done.74.refs_12_ = bf16[272,256]{1,0:T(8,128)(2,1)S(1)} collective-permute-done((bf16[272,256]{1,0:T(8,128)(2,1)S(1)}, bf16[272,256]{1,0:T(8,128)(2,1)S(1)}, u32[]{:S(2)}, u32[]{:S(2)}) %collective-permute-start.74) | collective-permute-done | bytes 139296 | tf_op jit(solution)/shard_map/ppermute | solution.py:39
  206.9 2.6 %last_gradient.1 = (f32[256,2048]{1,0:T(8,128)}, f32[256,256]{1,0:T(8,128)}, f32[1,128]{1,0:T(1,128)}) custom-call(s32[8]{0:T(128)S(1)} %stack.60.refs_0_.ids_ref, bf16[256,512]{1,0:T(8,128)(2,1)S(1)} %get-tuple-element.610.refs_1_, bf16[64,2048]{1,0:T(8,128)(2,1)S(1)} %get-tuple-element.615.refs_2_, bf16[64,2048]{1,0:T(8,128)(2,1)S(1)} %collective-permute-done.62.refs_3_, ...), custom_call_target="tpu_custom_call" | custom-call | tf_op jit(solution)/shard_map/last_gradient/pallas_call | solution.py:59
  (166 shorter events, 53.3 us)
Async XLA Ops:
  8.4 9.3 %collective-permute-start.33 = (bf16[208,512]{1,0:T(8,128)(2,1)S(1)}, bf16[208,512]{1,0:T(8,128)(2,1)S(1)}, u32[]{:S(2)}, u32[]{:S(2)}) collective-permute-start(bf16[208,512]{1,0:T(8,128)(2,1)S(1)} %join.2.refs_2_), channel_id=1, source_target_pairs={{12,13},{13,12},{14,15},{15,14},{28,29},{29,28},{30,31},{31,30}} | collective-permute-start | bytes 638984 | tf_op jit(solution)/shard_map/ppermute | solution.py:46
  11.3 15.0 %collective-permute-start.21 = (bf16[128,2048]{1,0:T(8,128)(2,1)S(1)}, bf16[128,2048]{1,0:T(8,128)(2,1)}, u32[]{:S(2)}, u32[]{:S(2)}) collective-permute-start(bf16[128,2048]{1,0:T(8,128)(2,1)S(1)} %get-tuple-element.748), channel_id=1, source_target_pairs={{0,1},{1,0},{2,3},{3,2},{4,5},{5,4},{6,7},{7,6},{8,9},{9,8},{10,11... | collective-permute-start | bytes 1572872 | tf_op jit(solution)/shard_map/ppermute | solution.py:26
  13.3 33.6 %collective-permute-start.24 = (bf16[128,2048]{1,0:T(8,128)(2,1)S(1)}, bf16[128,2048]{1,0:T(8,128)(2,1)}, u32[]{:S(2)}, u32[]{:S(2)}) collective-permute-start(bf16[128,2048]{1,0:T(8,128)(2,1)S(1)} %get-tuple-element.747), channel_id=1, source_target_pairs={{0,2},{1,3},{2,0},{3,1},{4,6},{5,7},{6,4},{7,5},{8,10},{9,11},{10,... | collective-permute-start | bytes 1572872 | tf_op jit(solution)/shard_map/ppermute | solution.py:26
  17.7 30.7 %collective-permute-start.29 = (bf16[128,2048]{1,0:T(8,128)(2,1)S(1)}, bf16[128,2048]{1,0:T(8,128)(2,1)}, u32[]{:S(2)}, u32[]{:S(2)}) collective-permute-start(bf16[128,2048]{1,0:T(8,128)(2,1)S(1)} %get-tuple-element.747), channel_id=1, source_target_pairs={{0,1},{1,0},{2,3},{3,2},{4,5},{5,4},{6,7},{7,6},{8,9},{9,8},{10,11... | collective-permute-start | bytes 1572872 | tf_op jit(solution)/shard_map/ppermute | solution.py:26
  18.8 26.5 %collective-permute-start.36 = (bf16[128,512]{1,0:T(8,128)(2,1)S(1)}, bf16[128,512]{1,0:T(8,128)(2,1)S(1)}, u32[]{:S(2)}, u32[]{:S(2)}) collective-permute-start(bf16[128,512]{1,0:T(8,128)(2,1)S(1)} %pick.2), channel_id=1, source_target_pairs={{12,0},{13,1},{14,2},{15,3},{28,16},{29,17},{30,18},{31,19}} | collective-permute-start | bytes 393224 | tf_op jit(solution)/shard_map/ppermute | solution.py:39
  21.5 27.0 %collective-permute-start.31 = (bf16[128,2048]{1,0:T(8,128)(2,1)S(1)}, bf16[128,2048]{1,0:T(8,128)(2,1)}, u32[]{:S(2)}, u32[]{:S(2)}) collective-permute-start(bf16[128,2048]{1,0:T(8,128)(2,1)S(1)} %get-tuple-element.748), channel_id=1, source_target_pairs={{0,2},{1,3},{2,0},{3,1},{4,6},{5,7},{6,4},{7,5},{8,10},{9,11},{10,... | collective-permute-start | bytes 1572872 | tf_op jit(solution)/shard_map/ppermute | solution.py:26
  26.2 22.7 %collective-permute-start.27 = (bf16[128,2048]{1,0:T(8,128)(2,1)}, bf16[128,2048]{1,0:T(8,128)(2,1)}, u32[]{:S(2)}, u32[]{:S(2)}) collective-permute-start(bf16[128,2048]{1,0:T(8,128)(2,1)} %collective-permute-done.21.refs_2_), channel_id=1, source_target_pairs={{0,16},{16,0},{1,17},{17,1},{2,18},{18,2},{3,19},{19,3},{4,20},{20... | collective-permute-start | bytes 1572872 | tf_op jit(solution)/shard_map/ppermute | solution.py:31
  45.3 9.5 %collective-permute-start.22 = (bf16[128,2048]{1,0:T(8,128)(2,1)}, bf16[128,2048]{1,0:T(8,128)(2,1)}, u32[]{:S(2)}, u32[]{:S(2)}) collective-permute-start(bf16[128,2048]{1,0:T(8,128)(2,1)} %collective-permute-done.21.refs_2_), channel_id=1, source_target_pairs={{0,2},{1,3},{2,0},{3,1},{4,6},{5,7},{6,4},{7,5},{8,10},{9,11},{10,... | collective-permute-start | bytes 1572872 | tf_op jit(solution)/shard_map/ppermute | solution.py:26
  46.8 9.5 %collective-permute-start.25 = (bf16[128,2048]{1,0:T(8,128)(2,1)}, bf16[128,2048]{1,0:T(8,128)(2,1)}, u32[]{:S(2)}, u32[]{:S(2)}) collective-permute-start(bf16[128,2048]{1,0:T(8,128)(2,1)} %collective-permute-done.24.refs_4_), channel_id=1, source_target_pairs={{0,1},{1,0},{2,3},{3,2},{4,5},{5,4},{6,7},{7,6},{8,9},{9,8},{10,11... | collective-permute-start | bytes 1572872 | tf_op jit(solution)/shard_map/ppermute | solution.py:26
  48.4 12.0 %collective-permute-start.28 = (bf16[128,2048]{1,0:T(8,128)(2,1)}, bf16[128,2048]{1,0:T(8,128)(2,1)}, u32[]{:S(2)}, u32[]{:S(2)}) collective-permute-start(bf16[128,2048]{1,0:T(8,128)(2,1)} %collective-permute-done.24.refs_4_), channel_id=1, source_target_pairs={{0,16},{16,0},{1,17},{17,1},{2,18},{18,2},{3,19},{19,3},{4,20},{20... | collective-permute-start | bytes 1572872 | tf_op jit(solution)/shard_map/ppermute | solution.py:31
  48.5 11.9 %collective-permute-start.30 = (bf16[128,2048]{1,0:T(8,128)(2,1)}, bf16[128,2048]{1,0:T(8,128)(2,1)}, u32[]{:S(2)}, u32[]{:S(2)}) collective-permute-start(bf16[128,2048]{1,0:T(8,128)(2,1)} %collective-permute-done.29.refs_6_), channel_id=1, source_target_pairs={{0,16},{16,0},{1,17},{17,1},{2,18},{18,2},{3,19},{19,3},{4,20},{20... | collective-permute-start | bytes 1572872 | tf_op jit(solution)/shard_map/ppermute | solution.py:31
  49.0 11.5 %collective-permute-start.32 = (bf16[128,2048]{1,0:T(8,128)(2,1)}, bf16[128,2048]{1,0:T(8,128)(2,1)}, u32[]{:S(2)}, u32[]{:S(2)}) collective-permute-start(bf16[128,2048]{1,0:T(8,128)(2,1)} %collective-permute-done.31.refs_8_), channel_id=1, source_target_pairs={{0,16},{16,0},{1,17},{17,1},{2,18},{18,2},{3,19},{19,3},{4,20},{20... | collective-permute-start | bytes 1572872 | tf_op jit(solution)/shard_map/ppermute | solution.py:31
  73.2 9.4 %collective-permute-start.39 = (bf16[64,2048]{1,0:T(8,128)(2,1)S(1)}, bf16[64,2048]{1,0:T(8,128)(2,1)S(1)}, u32[]{:S(2)}, u32[]{:S(2)}) collective-permute-start(bf16[64,2048]{1,0:T(8,128)(2,1)S(1)} %get-tuple-element.560.refs_5_.refs_2_), channel_id=1, source_target_pairs={{0,4},{1,5},{2,6},{3,7},{16,20},{17,21},{18,22},{19,23}} | collective-permute-start | bytes 786440 | tf_op jit(solution)/shard_map/ppermute | solution.py:39
  77.7 9.3 %collective-permute-start.38 = (bf16[64,2048]{1,0:T(8,128)(2,1)S(1)}, bf16[64,2048]{1,0:T(8,128)(2,1)S(1)}, u32[]{:S(2)}, u32[]{:S(2)}) collective-permute-start(bf16[64,2048]{1,0:T(8,128)(2,1)S(1)} %get-tuple-element.561.refs_6_), channel_id=1, source_target_pairs={{4,8},{5,9},{6,10},{7,11},{20,24},{21,25},{22,26},{23,27}} | collective-permute-start | bytes 786440 | tf_op jit(solution)/shard_map/ppermute | solution.py:39
  101.9 54.2 %collective-permute-start.56 = (bf16[64,2048]{1,0:T(8,128)(2,1)S(1)}, bf16[64,2048]{1,0:T(8,128)(2,1)S(1)}, u32[]{:S(2)}, u32[]{:S(2)}) collective-permute-start(bf16[64,2048]{1,0:T(8,128)(2,1)S(1)} %get-tuple-element.601), channel_id=1, source_target_pairs={{4,0},{5,1},{6,2},{7,3},{20,16},{21,17},{22,18},{23,19}} | collective-permute-start | bytes 786440 | tf_op jit(solution)/shard_map/ppermute | solution.py:39
  103.2 56.8 %collective-permute-start.70 = (bf16[144,1536]{1,0:T(8,128)(2,1)S(1)}, bf16[144,1536]{1,0:T(8,128)(2,1)S(1)}, u32[]{:S(2)}, u32[]{:S(2)}) collective-permute-start(bf16[144,1536]{1,0:T(8,128)(2,1)S(1)} %get-tuple-element.618), channel_id=1, source_target_pairs={{12,13},{13,12},{14,15},{15,14},{28,29},{29,28},{30,31},{31,30}} | collective-permute-start | bytes 1327112 | tf_op jit(solution)/shard_map/ppermute | solution.py:755
  105.6 55.9 %collective-permute-start.71 = (bf16[144,1536]{1,0:T(8,128)(2,1)S(1)}, bf16[144,1536]{1,0:T(8,128)(2,1)S(1)}, u32[]{:S(2)}, u32[]{:S(2)}) collective-permute-start(bf16[144,1536]{1,0:T(8,128)(2,1)S(1)} %get-tuple-element.619), channel_id=1, source_target_pairs={{12,14},{13,15},{14,12},{15,13},{28,30},{29,31},{30,28},{31,29}} | collective-permute-start | bytes 1327112 | tf_op jit(solution)/shard_map/ppermute | solution.py:755
  106.3 55.2 %collective-permute-start.72 = (bf16[144,1536]{1,0:T(8,128)(2,1)S(1)}, bf16[144,1536]{1,0:T(8,128)(2,1)S(1)}, u32[]{:S(2)}, u32[]{:S(2)}) collective-permute-start(bf16[144,1536]{1,0:T(8,128)(2,1)S(1)} %get-tuple-element.620), channel_id=1, source_target_pairs={{12,15},{13,14},{14,13},{15,12},{28,31},{29,30},{30,29},{31,28}} | collective-permute-start | bytes 1327112 | tf_op jit(solution)/shard_map/ppermute | solution.py:755
  112.9 44.5 %collective-permute-start.51 = (bf16[128,512]{1,0:T(8,128)(2,1)S(1)}, bf16[128,512]{1,0:T(8,128)(2,1)S(1)}, u32[]{:S(2)}, u32[]{:S(2)}) collective-permute-start(bf16[128,512]{1,0:T(8,128)(2,1)S(1)} %get-tuple-element.594.refs_8_.refs_1_), channel_id=1, source_target_pairs={{0,16},{16,0},{1,17},{17,1},{2,18},{18,2},{3,19},{19,3},{4,20},{20... | collective-permute-start | bytes 393224 | tf_op jit(solution)/shard_map/ppermute | solution.py:31
  157.5 9.7 %collective-permute-start.58 = (bf16[64,2048]{1,0:T(8,128)(2,1)S(1)}, bf16[64,2048]{1,0:T(8,128)(2,1)S(1)}, u32[]{:S(2)}, u32[]{:S(2)}) collective-permute-start(bf16[64,2048]{1,0:T(8,128)(2,1)S(1)} %get-tuple-element.609.refs_9_), channel_id=1, source_target_pairs={{0,1},{1,0},{2,3},{3,2},{4,5},{5,4},{6,7},{7,6},{8,9},{9,8},{10,11... | collective-permute-start | bytes 786440 | tf_op jit(solution)/shard_map/ppermute | solution.py:26
  160.0 14.1 %collective-permute-start.59 = (bf16[64,2048]{1,0:T(8,128)(2,1)S(1)}, bf16[64,2048]{1,0:T(8,128)(2,1)S(1)}, u32[]{:S(2)}, u32[]{:S(2)}) collective-permute-start(bf16[64,2048]{1,0:T(8,128)(2,1)S(1)} %get-tuple-element.609.refs_9_), channel_id=1, source_target_pairs={{0,2},{1,3},{2,0},{3,1},{4,6},{5,7},{6,4},{7,5},{8,10},{9,11},{10,... | collective-permute-start | bytes 786440 | tf_op jit(solution)/shard_map/ppermute | solution.py:26
  161.5 12.5 %collective-permute-start.60 = (bf16[64,2048]{1,0:T(8,128)(2,1)S(1)}, bf16[64,2048]{1,0:T(8,128)(2,1)S(1)}, u32[]{:S(2)}, u32[]{:S(2)}) collective-permute-start(bf16[64,2048]{1,0:T(8,128)(2,1)S(1)} %get-tuple-element.609.refs_9_), channel_id=1, source_target_pairs={{0,3},{1,2},{2,1},{3,0},{4,7},{5,6},{6,5},{7,4},{8,11},{9,10},{10,... | collective-permute-start | bytes 786440 | tf_op jit(solution)/shard_map/ppermute | solution.py:26
  162.9 13.3 %collective-permute-start.61 = (bf16[64,2048]{1,0:T(8,128)(2,1)S(1)}, bf16[64,2048]{1,0:T(8,128)(2,1)S(1)}, u32[]{:S(2)}, u32[]{:S(2)}) collective-permute-start(bf16[64,2048]{1,0:T(8,128)(2,1)S(1)} %get-tuple-element.611), channel_id=1, source_target_pairs={{4,0},{5,1},{6,2},{7,3},{20,16},{21,17},{22,18},{23,19}} | collective-permute-start | bytes 786440 | tf_op jit(solution)/shard_map/ppermute | solution.py:39
  164.9 17.0 %collective-permute-start.73 = (bf16[272,1024]{1,0:T(8,128)(2,1)S(1)}, bf16[272,1024]{1,0:T(8,128)(2,1)S(1)}, u32[]{:S(2)}, u32[]{:S(2)}) collective-permute-start(bf16[272,1024]{1,0:T(8,128)(2,1)S(1)} %get-tuple-element.622), channel_id=1, source_target_pairs={{0,16},{16,0},{1,17},{17,1},{2,18},{18,2},{3,19},{19,3},{4,20},{20... | collective-permute-start | bytes 1671176 | tf_op jit(solution)/shard_map/ppermute | solution.py:31
  175.9 31.1 %collective-permute-start.69 = (bf16[256,2048]{1,0:T(8,128)(2,1)S(1)}, bf16[256,2048]{1,0:T(8,128)(2,1)S(1)}, u32[]{:S(2)}, u32[]{:S(2)}) collective-permute-start(bf16[256,2048]{1,0:T(8,128)(2,1)S(1)} %get-tuple-element.617), channel_id=1, source_target_pairs={{0,16},{16,0},{1,17},{17,1},{2,18},{18,2},{3,19},{19,3},{4,20},{20... | collective-permute-start | bytes 3145736 | tf_op jit(solution)/shard_map/ppermute | solution.py:31
  179.3 12.4 %collective-permute-start.63 = (bf16[64,2048]{1,0:T(8,128)(2,1)S(1)}, bf16[64,2048]{1,0:T(8,128)(2,1)S(1)}, u32[]{:S(2)}, u32[]{:S(2)}) collective-permute-start(bf16[64,2048]{1,0:T(8,128)(2,1)S(1)} %get-tuple-element.615.refs_2_), channel_id=1, source_target_pairs={{0,2},{1,3},{2,0},{3,1},{4,6},{5,7},{6,4},{7,5},{8,10},{9,11},{10,... | collective-permute-start | bytes 786440 | tf_op jit(solution)/shard_map/ppermute | solution.py:26
  180.3 13.1 %collective-permute-start.64 = (bf16[64,2048]{1,0:T(8,128)(2,1)S(1)}, bf16[64,2048]{1,0:T(8,128)(2,1)S(1)}, u32[]{:S(2)}, u32[]{:S(2)}) collective-permute-start(bf16[64,2048]{1,0:T(8,128)(2,1)S(1)} %get-tuple-element.615.refs_2_), channel_id=1, source_target_pairs={{0,3},{1,2},{2,1},{3,0},{4,7},{5,6},{6,5},{7,4},{8,11},{9,10},{10,... | collective-permute-start | bytes 786440 | tf_op jit(solution)/shard_map/ppermute | solution.py:26
  181.8 11.5 %collective-permute-start.65 = (bf16[64,2048]{1,0:T(8,128)(2,1)S(1)}, bf16[64,2048]{1,0:T(8,128)(2,1)S(1)}, u32[]{:S(2)}, u32[]{:S(2)}) collective-permute-start(bf16[64,2048]{1,0:T(8,128)(2,1)S(1)} %get-tuple-element.615.refs_2_), channel_id=1, source_target_pairs={{0,16},{16,0},{1,17},{17,1},{2,18},{18,2},{3,19},{19,3},{4,20},{20... | collective-permute-start | bytes 786440 | tf_op jit(solution)/shard_map/ppermute | solution.py:31
  187.5 17.8 %collective-permute-start.74 = (bf16[272,256]{1,0:T(8,128)(2,1)S(1)}, bf16[272,256]{1,0:T(8,128)(2,1)S(1)}, u32[]{:S(2)}, u32[]{:S(2)}) collective-permute-start(bf16[272,256]{1,0:T(8,128)(2,1)S(1)} %get-tuple-element.623), channel_id=1, source_target_pairs={{12,0},{13,1},{14,2},{15,3},{28,16},{29,17},{30,18},{31,19}} | collective-permute-start | bytes 417800 | tf_op jit(solution)/shard_map/ppermute | solution.py:39
  191.7 13.7 %collective-permute-start.75 = (bf16[272,256]{1,0:T(8,128)(2,1)S(1)}, bf16[272,256]{1,0:T(8,128)(2,1)S(1)}, u32[]{:S(2)}, u32[]{:S(2)}) collective-permute-start(bf16[272,256]{1,0:T(8,128)(2,1)S(1)} %get-tuple-element.624), channel_id=1, source_target_pairs={{12,4},{13,5},{14,6},{15,7},{28,20},{29,21},{30,22},{31,23}} | collective-permute-start | bytes 417800 | tf_op jit(solution)/shard_map/ppermute | solution.py:39
  193.4 12.7 %collective-permute-start.66 = (bf16[64,2048]{1,0:T(8,128)(2,1)S(1)}, bf16[64,2048]{1,0:T(8,128)(2,1)S(1)}, u32[]{:S(2)}, u32[]{:S(2)}) collective-permute-start(bf16[64,2048]{1,0:T(8,128)(2,1)S(1)} %collective-permute-done.62.refs_3_), channel_id=1, source_target_pairs={{0,16},{16,0},{1,17},{17,1},{2,18},{18,2},{3,19},{19,3},{4,20},{20... | collective-permute-start | bytes 786440 | tf_op jit(solution)/shard_map/ppermute | solution.py:31
  193.4 12.7 %collective-permute-start.67 = (bf16[64,2048]{1,0:T(8,128)(2,1)S(1)}, bf16[64,2048]{1,0:T(8,128)(2,1)S(1)}, u32[]{:S(2)}, u32[]{:S(2)}) collective-permute-start(bf16[64,2048]{1,0:T(8,128)(2,1)S(1)} %collective-permute-done.63.refs_4_), channel_id=1, source_target_pairs={{0,16},{16,0},{1,17},{17,1},{2,18},{18,2},{3,19},{19,3},{4,20},{20... | collective-permute-start | bytes 786440 | tf_op jit(solution)/shard_map/ppermute | solution.py:31
  (33 other events, 236.4 us)
